TPU v7x, 32 devices: a whole 2x2x4 slice. The times are simulated.
32 devices in a mesh: section: 2 (over x), shard: 4 (over z), rep: 4 (over y, core).
Axes of the slice: x: 2, y: 2, z: 4, core: 2. Of those that a mesh axis runs over, the one named last changes fastest.
Arguments:
- latents: bfloat16 [32, 256, 1152], P(('shard', 'rep')), may hold values from -81 to 81
- cond: bfloat16 [32, 1152], P(('shard', 'rep')), may hold values from -6 to 6
- modulation_weight: bfloat16 [2, 1152, 6912], P('section', 'shard'), may hold values from -0.1875 to 0.1875
- query_key_value_weight: bfloat16 [2, 1152, 3456], P('section', 'shard'), may hold values from -0.1875 to 0.1875
- attention_output_weight: bfloat16 [2, 1152, 1152], P('section', 'shard'), may hold values from -1.5 to 1.5
- feed_first_weight: bfloat16 [2, 1152, 4608], P('section', 'shard'), may hold values from -0.1875 to 0.1875
- feed_second_weight: bfloat16 [2, 4608, 1152], P('section', 'shard'), may hold values from -0.09375 to 0.09375
- cotangent: bfloat16 [32, 256, 1152], P(('shard', 'rep')), may hold values from -6 to 6
Outputs:
- boundary: float32 [2, 32, 256, 1152], P('section', ('shard', 'rep'))
- grad_cond: float32 [32, 1152], P(('shard', 'rep'))
- grad_ada: float32 [2, 1152, 6912], P('section', 'shard')
- grad_qkv: float32 [2, 1152, 3456], P('section', 'shard')
- grad_out: float32 [2, 1152, 1152], P('section', 'shard')
- grad_fc1: float32 [2, 1152, 4608], P('section', 'shard')
- grad_fc2: float32 [2, 4608, 1152], P('section', 'shard')
All inputs are finite; a program needn't handle non-finite values.
Results may differ from a plain program's by a relative error of at most 0.03.
Values may be sent and summed in bfloat16 or wider, within the bound.
A program may use at most 384 MiB of HBM per device.

v0:
```python
import functools

import jax
import jax.numpy as jnp
from jax import lax
from jax.experimental import pallas as pl
from jax.experimental.pallas import tpu as pltpu
from jax.sharding import PartitionSpec as P


D = 1152
HEADS = 16
HEAD_DIM = 72
LANES = 128


epsilon = 1e-06
low = jnp.bfloat16


NT=(((1,),(1,)),((),())); TN=(((0,),(0,)),((),()))
def dot(a,b,dims=(((1,),(0,)),((),()))):
    return lax.dot_general(a,b,dims,preferred_element_type=jnp.float32)
def windows():
    for head in range(HEADS):
        start=head*HEAD_DIM; stop=start+HEAD_DIM
        first=start//LANES*LANES; last=-(-stop//LANES)*LANES
        yield first,last,start-first,stop-first
def head_mask(rows,first,last,begin,end):
    lane=lax.broadcasted_iota(jnp.int32,(rows,last-first),1)
    return (lane>=begin)&(lane<end)
def attention_kernel(project_ref,out_ref):
    rows=out_ref.shape[0]
    for first,last,begin,end in windows():
        mask=head_mask(rows,first,last,begin,end)
        q=project_ref[:,first:last]; k=project_ref[:,D+first:D+last]; v=project_ref[:,2*D+first:2*D+last]
        q=jnp.where(mask,q,jnp.zeros_like(q))
        s=dot(q,k,NT)*(HEAD_DIM**-0.5)
        e=jnp.exp(s-jnp.max(s,axis=1,keepdims=True))
        p=(e/jnp.sum(e,axis=1,keepdims=True)).astype(low)
        o=dot(p,v).astype(low)
        out_ref[:,first:last]=jnp.where(mask,o,out_ref[:,first:last])
def attention_back_kernel(project_ref,grad_ref,out_ref):
    rows=grad_ref.shape[0]; factor=HEAD_DIM**-0.5
    for first,last,begin,end in windows():
        mask=head_mask(rows,first,last,begin,end)
        q=project_ref[:,first:last]; k=project_ref[:,D+first:D+last]; v=project_ref[:,2*D+first:2*D+last]
        g=grad_ref[:,first:last]
        s=dot(jnp.where(mask,k,jnp.zeros_like(k)),q,NT)*factor
        e=jnp.exp(s-jnp.max(s,axis=0,keepdims=True))
        p=e/jnp.sum(e,axis=0,keepdims=True)
        dp=dot(jnp.where(mask,v,jnp.zeros_like(v)),g,NT)
        ds=(p*(dp-jnp.sum(dp*p,axis=0,keepdims=True))).astype(low)
        dq=(dot(ds,k,TN)*factor).astype(low)
        dk=(dot(ds,q)*factor).astype(low)
        dv=dot(p.astype(low),g).astype(low)
        for base,piece in ((0,dq),(D,dk),(2*D,dv)):
            here=slice(base+first,base+last)
            out_ref[:,here]=jnp.where(mask,piece,out_ref[:,here])
def attention(project,length):
    tokens=project.shape[0]
    return pl.pallas_call(attention_kernel,grid=(tokens//length,),
        in_specs=[pl.BlockSpec((length,3*D),lambda i:(i,0))],out_specs=pl.BlockSpec((length,D),lambda i:(i,0)),
        out_shape=jax.ShapeDtypeStruct((tokens,D),low),
        cost_estimate=pl.CostEstimate(flops=4*tokens*length*D,bytes_accessed=8*tokens*D,transcendentals=HEADS*tokens*length))(project)
def attention_back(project,grad,length):
    tokens=project.shape[0]
    return pl.pallas_call(attention_back_kernel,grid=(tokens//length,),
        in_specs=[pl.BlockSpec((length,3*D),lambda i:(i,0)),pl.BlockSpec((length,D),lambda i:(i,0))],out_specs=pl.BlockSpec((length,3*D),lambda i:(i,0)),
        out_shape=jax.ShapeDtypeStruct((tokens,3*D),low),
        cost_estimate=pl.CostEstimate(flops=10*tokens*length*D,bytes_accessed=14*tokens*D,transcendentals=HEADS*tokens*length))(project,grad)

C0=0.7978845608028654; C1=0.044715
def act_of(u): return (0.5*u*(1.0+jnp.tanh(C0*(u+C1*(u*u*u))))).astype(low)
def slope_of(u):
    sq=u*u
    t=jnp.tanh(C0*(u+C1*(sq*u)))
    return 0.5*(1.0+t)+0.5*u*(1.0-t*t)*(C0*(1.0+3.0*C1*sq))
def mlp_kernel(chunk,x_ref,middle_ref,gate_ref,w1_ref,w2_ref,u_ref,h_ref,f_ref,y_ref,y_low_ref):
    tile=w1_ref.shape[1]
    parts=[slice(a,a+chunk) for a in range(0,tile,chunk)]
    first=pl.program_id(0)==0
    @pl.when(first)
    def _(): f_ref[...]=jnp.zeros_like(f_ref)
    def front(p):
        u=dot(x_ref[...],w1_ref[:,p]); u_ref[:,p]=u
        return u
    def back(p,u):
        h=act_of(u); h_ref[:,p]=h
        f_ref[...]+=dot(h,w2_ref[p,:])
    prev=None
    for p in parts:
        u=front(p)
        if prev is not None: back(*prev)
        prev=(p,u)
    back(*prev)
    @pl.when(pl.program_id(0)==pl.num_programs(0)-1)
    def _():
        y=middle_ref[...]+gate_ref[...]*f_ref[...]
        y_ref[...]=y
        y_low_ref[...]=y.astype(low)
def mlp_back_kernel(chunk,g_ref,w1_ref,w2_ref,u_ref,du_ref,dx_ref):
    tile=w1_ref.shape[1]
    parts=[slice(a,a+chunk) for a in range(0,tile,chunk)]
    first=pl.program_id(0)==0
    @pl.when(first)
    def _(): dx_ref[...]=jnp.zeros_like(dx_ref)
    def front(p): return dot(g_ref[...],w2_ref[p,:],NT)
    def mid(p,dh):
        du=(dh*slope_of(u_ref[:,p])).astype(low); du_ref[:,p]=du
        return du
    prev=None
    for p in parts:
        dh=front(p)
        if prev is not None: dx_ref[...]+=dot(mid(*prev),w1_ref[:,prev[0]],NT)
        prev=(p,dh)
    dx_ref[...]+=dot(mid(*prev),w1_ref[:,prev[0]],NT)
def mlp(x,middle,gate,w1,w2,tile=1536,chunk=512):
    t,d=x.shape; ff=w1.shape[1]
    whole=pl.BlockSpec((t,d),lambda i:(0,0))
    cols=pl.BlockSpec((t,tile),lambda i:(0,i))
    made=lambda width,dtype: jax.ShapeDtypeStruct((t,width),dtype)
    return pl.pallas_call(functools.partial(mlp_kernel,chunk),grid=(ff//tile,),
        in_specs=[whole,whole,pl.BlockSpec((1,d),lambda i:(0,0)),pl.BlockSpec((d,tile),lambda i:(0,i)),pl.BlockSpec((tile,d),lambda i:(i,0))],
        out_specs=[cols,cols,whole,whole,whole],
        out_shape=[made(ff,jnp.float32),made(ff,low),made(d,jnp.float32),made(d,jnp.float32),made(d,low)],
        cost_estimate=pl.CostEstimate(flops=4*t*d*ff,bytes_accessed=4*d*ff+6*t*ff+16*t*d,transcendentals=t*ff))(x,middle,gate,w1,w2)
def mlp_back(g,w1,w2,u,tile=1536,chunk=512):
    t,d=g.shape; ff=w1.shape[1]
    whole=pl.BlockSpec((t,d),lambda i:(0,0))
    cols=pl.BlockSpec((t,tile),lambda i:(0,i))
    return pl.pallas_call(functools.partial(mlp_back_kernel,chunk),grid=(ff//tile,),
        in_specs=[whole,pl.BlockSpec((d,tile),lambda i:(0,i)),pl.BlockSpec((tile,d),lambda i:(i,0)),cols],
        out_specs=[cols,whole],
        out_shape=[jax.ShapeDtypeStruct((t,ff),low),jax.ShapeDtypeStruct((t,d),jnp.float32)],
        cost_estimate=pl.CostEstimate(flops=4*t*d*ff,bytes_accessed=4*d*ff+6*t*ff+6*t*d,transcendentals=t*ff))(g,w1,w2,u)


def center_scale(values):
    center = values - jnp.mean(values, axis=-1, keepdims=True)
    scale = lax.rsqrt(jnp.mean(center * center, axis=-1, keepdims=True) + epsilon)
    return center * scale, scale


def norm_back(normed, scale, grad):
    mean_grad = jnp.mean(grad, axis=-1, keepdims=True)
    mean_dot = jnp.mean(grad * normed, axis=-1, keepdims=True)
    return (grad - mean_grad - normed * mean_dot) * scale


def matmul(left, right):
    return jnp.dot(left, right, preferred_element_type=jnp.float32)


def matmul_t(left, right):
    return lax.dot_general(
        left, right, (((1,), (1,)), ((), ())), preferred_element_type=jnp.float32
    )


def forward_layer(input_rows, modulation, weights):
    query_key_value_weight, attention_output_weight, feed_first_weight, feed_second_weight = weights
    batch_size, length, model_width = input_rows.shape
    tokens = batch_size * length
    shift_one, scale_one, gate_one, shift_two, scale_two, gate_two = modulation
    normed_one, _ = center_scale(input_rows)
    first_in = (normed_one * (1.0 + scale_one) + shift_one).astype(low).reshape(tokens, model_width)
    project = matmul(first_in, query_key_value_weight).astype(low)
    attended = attention(project, length)
    branch = matmul(attended, attention_output_weight).reshape(batch_size, length, model_width)
    middle_state = input_rows + gate_one * branch
    normed_two, _ = center_scale(middle_state)
    second_in = (
        (normed_two * (1.0 + scale_two) + shift_two).astype(low).reshape(tokens, model_width)
    )
    shape = (batch_size, length, model_width)
    hidden_pre, hidden, feed_out, result, result_low = mlp(
        second_in,
        middle_state.reshape(tokens, model_width),
        gate_two.reshape(1, model_width),
        feed_first_weight,
        feed_second_weight,
    )
    feed_out, result, result_low = (
        value.reshape(shape) for value in (feed_out, result, result_low)
    )
    kept = (
        first_in,
        project,
        attended,
        branch,
        middle_state,
        second_in,
        hidden_pre,
        hidden,
        feed_out,
    )
    return result, result_low, kept


def backward_layer(input_rows, modulation, weights, kept, grad_result):
    query_key_value_weight, attention_output_weight, feed_first_weight, feed_second_weight = weights
    (
        first_in,
        project,
        attended,
        branch,
        middle_state,
        second_in,
        hidden_pre,
        hidden,
        feed_out,
    ) = kept
    batch_size, length, model_width = input_rows.shape
    tokens = batch_size * length
    _, scale_one, gate_one, _, scale_two, gate_two = modulation
    grad_gate_two = jnp.sum(grad_result * feed_out, axis=1)
    grad_feed = (gate_two * grad_result).astype(low).reshape(tokens, model_width)
    grad_pre, grad_second = mlp_back(
        grad_feed, feed_first_weight, feed_second_weight, hidden_pre
    )
    grad_second = grad_second.reshape(batch_size, length, model_width)
    normed_two, inv_two = center_scale(middle_state)
    grad_shift_two = jnp.sum(grad_second, axis=1)
    grad_scale_two = jnp.sum(grad_second * normed_two, axis=1)
    grad_middle = grad_result + norm_back(normed_two, inv_two, grad_second * (1.0 + scale_two))
    grad_gate_one = jnp.sum(grad_middle * branch, axis=1)
    grad_branch = (gate_one * grad_middle).astype(low).reshape(tokens, model_width)
    grad_att = matmul_t(grad_branch, attention_output_weight).astype(low)
    grad_project = attention_back(project, grad_att, length)
    grad_first = matmul_t(grad_project, query_key_value_weight).reshape(
        batch_size, length, model_width
    )
    normed_one, inv_one = center_scale(input_rows)
    grad_shift_one = jnp.sum(grad_first, axis=1)
    grad_scale_one = jnp.sum(grad_first * normed_one, axis=1)
    grad_inputs = grad_middle + norm_back(normed_one, inv_one, grad_first * (1.0 + scale_one))
    grad_mod = jnp.concatenate(
        [
            grad_shift_one,
            grad_scale_one,
            grad_gate_one,
            grad_shift_two,
            grad_scale_two,
            grad_gate_two,
        ],
        axis=-1,
    ).astype(low)
    pairs = (
        (hidden, grad_feed),
        (second_in, grad_pre),
        (attended, grad_branch),
        (first_in, grad_project),
    )
    return grad_inputs, grad_mod, pairs


def bits_of(count):
    bits = count.bit_length() - 1
    assert 1 << bits == count
    return bits


def swap(value, axis, bit):
    count = lax.axis_size(axis)
    return lax.ppermute(value, axis, [(i, i ^ (1 << bit)) for i in range(count)])


def reduce_rows(left, right, reps_first):
    shard_bits = bits_of(lax.axis_size("shard"))
    rep_bits = bits_of(lax.axis_size("rep"))
    shard_stages = [("shard", bit) for bit in range(shard_bits)]
    rep_stages = [("rep", bit) for bit in range(rep_bits)]
    if reps_first:
        stages = rep_stages + shard_stages
    else:
        stages = rep_stages[:1] + shard_stages + rep_stages[1:]
    names = [("shard", bit) for bit in reversed(range(shard_bits))]
    names += [("rep", bit) for bit in reversed(range(rep_bits))]
    tokens, depth = left.shape
    inner = depth >> len(names)
    part = None
    for axis, bit in stages:
        place = names.index((axis, bit))
        mine = (lax.axis_index(axis) >> bit) & 1
        if part is None:
            spread = left.T.reshape((2,) * len(names) + (inner, tokens))
            away = lax.dynamic_index_in_dim(spread, 1 - mine, place, keepdims=False)
            stay = lax.dynamic_index_in_dim(spread, mine, place, keepdims=False)
            away = matmul(away.reshape(-1, tokens), right).astype(low)
            came = swap(away, axis, bit)
            part = (matmul(stay.reshape(-1, tokens), right) + came.astype(jnp.float32)).astype(low)
            names.pop(place)
            part = part.reshape((2,) * len(names) + (inner, right.shape[1]))
        else:
            away = lax.dynamic_index_in_dim(part, 1 - mine, place, keepdims=False)
            stay = lax.dynamic_index_in_dim(part, mine, place, keepdims=False)
            came = swap(away, axis, bit)
            part = (stay.astype(jnp.float32) + came.astype(jnp.float32)).astype(low)
            names.pop(place)
    whole = lax.all_gather(part, "rep", axis=0, tiled=True)
    return whole.astype(jnp.float32)


def exchange_shards(blocks):
    count = lax.axis_size("shard")
    me = lax.axis_index("shard")
    came = [lax.dynamic_index_in_dim(blocks, me, 0, keepdims=False)]
    for step in range(1, count):
        block = lax.dynamic_index_in_dim(blocks, (me + step) % count, 0, keepdims=False)
        came.append(
            lax.ppermute(block, "shard", [(i, (i + step) % count) for i in range(count)])
        )
    return came


MESH=pl.DeviceIdType.MESH

def gather_kernel(shards,reps,count,*refs):
    ins=refs[:count]; outs=refs[count:2*count]; bounce=refs[2*count:3*count]
    line_send,line_recv,rep_send,rep_recv,local_in,local_out=refs[3*count:]
    s=lax.axis_index("shard"); r=lax.axis_index("rep")
    bits=reps.bit_length()-1
    barrier=pltpu.get_barrier_semaphore()
    for side in (-1,1):
        there=(s+side>=0)&(s+side<shards)
        @pl.when(there)
        def _():
            pl.semaphore_signal(barrier,inc=1,device_id={"shard":s+side},device_id_type=MESH)
    for bit in range(bits):
        pl.semaphore_signal(barrier,inc=1,device_id={"rep":r^(1<<bit)},device_id_type=MESH)
    for c in range(count):
        pltpu.make_async_copy(ins[c],bounce[c],local_in.at[c]).start()
    pl.semaphore_wait(barrier,bits+jnp.minimum(s,1)+jnp.minimum(shards-1-s,1))
    sides=((0,1),(1,-1))

    def line(way,step,hop,c,owner):
        src=ins[c].at[r] if hop==0 else outs[c].at[owner,r]
        return pltpu.make_async_remote_copy(src_ref=src,dst_ref=outs[c].at[owner,r],
            send_sem=line_send.at[way,hop,c],recv_sem=line_recv.at[way,hop,c],
            device_id={"shard":s+step},device_id_type=MESH)
    def side_copy(bit,mask,c,owner):
        piece=outs[c].at[owner,r^mask]
        return pltpu.make_async_remote_copy(src_ref=piece,dst_ref=piece,
            send_sem=rep_send.at[bit,mask,owner,c],recv_sem=rep_recv.at[mask|(1<<bit),owner,c],
            device_id={"rep":r^(1<<bit)},device_id_type=MESH)
    def low_bit(mask): return bits if mask==0 else (mask&-mask).bit_length()-1
    def arrived(mask,c,owner):
        bit=low_bit(mask)
        piece=outs[c].at[owner,r^mask]
        pltpu.make_async_remote_copy(src_ref=piece,dst_ref=piece,send_sem=rep_send.at[bit,mask^(1<<bit),owner,c],
            recv_sem=rep_recv.at[mask,owner,c],device_id={"rep":r^(1<<bit)},device_id_type=MESH).wait_recv()
    for c in range(count):
        for way,step in sides:
            @pl.when((s+step>=0)&(s+step<shards))
            def _(): line(way,step,0,c,s).start()
    for c in range(count):
        pltpu.make_async_copy(ins[c],bounce[c],local_in.at[c]).wait()
        pltpu.make_async_copy(bounce[c],outs[c].at[s],local_out.at[c]).start()
    events=[(hop,c) for hop in range(1,shards) for c in range(count)]
    relays=[m for m in range(1,reps) if low_bit(m)>0]
    depth=max([m.bit_count() for m in relays],default=0)
    for index in range(len(events)+depth):
        if index<len(events):
            hop,c=events[index]
            for way,step in sides:
                owner=s-step*hop
                @pl.when((owner>=0)&(owner<shards))
                def _():
                    line(way,step,hop-1,c,owner).wait_recv()
                    if hop+1<shards:
                        @pl.when((s+step>=0)&(s+step<shards))
                        def _(): line(way,step,hop,c,owner).start()
                    for bit in reversed(range(bits)):
                        side_copy(bit,0,c,owner).start()
        for mask in relays:
            late=index-mask.bit_count()
            if 0<=late<len(events):
                hop,c=events[late]
                for way,step in sides:
                    owner=s-step*hop
                    @pl.when((owner>=0)&(owner<shards))
                    def _():
                        arrived(mask,c,owner)
                        for bit in reversed(range(low_bit(mask))):
                            side_copy(bit,mask,c,owner).start()
    for hop,c in events:
        for way,step in sides:
            owner=s-step*hop
            @pl.when((owner>=0)&(owner<shards))
            def _():
                for mask in range(1,reps):
                    if low_bit(mask)==0: arrived(mask,c,owner)
                for mask in range(reps):
                    for bit in range(low_bit(mask)): side_copy(bit,mask,c,owner).wait_send()
                if hop+1<shards:
                    @pl.when((s+step>=0)&(s+step<shards))
                    def _(): line(way,step,hop,c,owner).wait_send()
    for c in range(count):
        for way,step in sides:
            @pl.when((s+step>=0)&(s+step<shards))
            def _(): line(way,step,0,c,s).wait_send()
        pltpu.make_async_copy(bounce[c],outs[c].at[s],local_out.at[c]).wait()

def gather_all(weights):
    shards=lax.axis_size("shard"); reps=lax.axis_size("rep"); bits=reps.bit_length()-1
    assert 1<<bits==reps
    count=len(weights)
    views=[w.reshape(reps,w.shape[0]//reps,w.shape[1]) for w in weights]
    any_=pl.BlockSpec(memory_space=pl.ANY)
    outs=pl.pallas_call(functools.partial(gather_kernel,shards,reps,count),
        in_specs=[any_]*count,out_specs=[any_]*count,
        out_shape=[jax.ShapeDtypeStruct((shards,)+v.shape,v.dtype) for v in views],
        scratch_shapes=[pltpu.VMEM(v.shape,v.dtype) for v in views]+[
            pltpu.SemaphoreType.DMA((2,shards-1,count)),pltpu.SemaphoreType.DMA((2,shards-1,count)),
            pltpu.SemaphoreType.DMA((bits,reps,shards,count)),pltpu.SemaphoreType.DMA((reps,shards,count)),
            pltpu.SemaphoreType.DMA((count,)),pltpu.SemaphoreType.DMA((count,))],
        compiler_params=pltpu.CompilerParams(collective_id=1,has_side_effects=True),
        )(*views)
    return tuple(o.reshape(shards*w.shape[0],w.shape[1]) for o,w in zip(outs,weights))


NAMES=("s1","s0","r1","r0")
REP_FIRST=("r0","r1","s0","s1")
SHARD_FIRST=("r0","s0","s1","r1")
KINDS=(REP_FIRST,SHARD_FIRST,REP_FIRST)
WIDTH=D//3
LAGS=(1,3,3,2)

def block_sources(first_t,second_t,att_t,hidden_t,feed,pre,branch,project):
    pairs=[(hidden_t.at[:,j],feed) for j in range(4)]
    pairs+=[(second_t,pre.at[:,j*D:(j+1)*D]) for j in range(4)]
    pairs+=[(att_t,branch)]
    pairs+=[(first_t,project.at[:,j*D:(j+1)*D]) for j in range(3)]
    return pairs

def reduce_kernel(blocks,*refs):
    ins=(refs[:8],refs[8:16]); note,ada,outs,notes,act_out=refs[16],refs[17],refs[18:22],refs[22],refs[23]
    (left,right,left_sem,right_sem,part,came,send_sem,recv_sem,kept,final,
     final_sem,near_send,near_recv,far_send,far_recv,fwd_send,fwd_recv,note_send,note_recv,
     notes_in,ada_in,ada_sem,_,blocks_out,blocks_in,act_send,act_recv)=unpack(refs[24:])
    c=lax.axis_index("section")
    s=lax.axis_index("shard"); r=lax.axis_index("rep")
    bit={"s1":s//2,"s0":lax.rem(s,2),"r1":r//2,"r0":lax.rem(r,2)}
    peer={"s1":{"shard":lax.rem(s+2,4)},"s0":{"shard":s+1-2*lax.rem(s,2)},
          "r1":{"rep":lax.rem(r+2,4)},"r0":{"rep":r+1-2*lax.rem(r,2)}}
    across=lax.rem(r+2,4)
    barrier=pltpu.get_barrier_semaphore()
    others=[(a,b) for a in range(4) for b in range(4) if a or b]
    def note_copy(index,a,b):
        return pltpu.make_async_remote_copy(src_ref=note,dst_ref=notes_in.at[s*4+r],send_sem=note_send.at[index],recv_sem=note_recv.at[index],
            device_id={"shard":s^a,"rep":r^b},device_id_type=MESH)
    for a,b in others:
        pl.semaphore_signal(barrier,inc=1,device_id={"shard":s^a,"rep":r^b},device_id_type=MESH)
    for a in range(4):
        pl.semaphore_signal(barrier,inc=1,device_id={"section":1-c,"shard":s^a},device_id_type=MESH)
    sources=[block_sources(*half) for half in ins]
    span=left.shape[3]//2
    def load(index,slot):
        for here in range(blocks):
            @pl.when(index==here)
            def _():
                for half in range(2):
                    a,b=sources[half][here]
                    place=pl.ds(half*span,span)
                    pltpu.make_async_copy(a,left.at[slot,:,:,place],left_sem.at[slot]).start()
                    pltpu.make_async_copy(b,right.at[slot,place],right_sem.at[slot]).start()
    load(0,0)
    pltpu.make_async_copy(ada,ada_in,ada_sem).start()
    pl.semaphore_wait(barrier,len(others)+4)
    for index,(a,b) in enumerate(others): note_copy(index,a,b).start()
    notes_in[s*4+r]=note[...]
    def act_copy(index,a,other):
        section=1-c if other else c
        return pltpu.make_async_remote_copy(src_ref=blocks_out.at[s^a],dst_ref=blocks_in.at[c,s],send_sem=act_send.at[index],
            recv_sem=act_recv.at[index],device_id={"section":section,"shard":s^a},device_id_type=MESH)
    act_peers=[(a,other) for a in range(4) for other in (False,True) if a or other]
    def share_notes():
        for index,(a,b) in enumerate(others): note_copy(index,a,b).wait()
        pltpu.make_async_copy(ada,ada_in,ada_sem).wait()
        wide=lambda index: notes_in[index].astype(jnp.float32)
        notes_out=jnp.concatenate([wide(index) for index in range(16)],axis=0).astype(low)
        notes[...]=notes_out
        mine=jnp.concatenate([wide(shard*4+r)[:,:6*D] for shard in range(4)],axis=0).astype(low)
        grads=lax.dot_general(mine,ada_in[...],(((1,),(1,)),((),())),preferred_element_type=jnp.float32)
        span=grads.shape[0]//4
        for shard in range(4): blocks_out[shard]=grads[shard*span:(shard+1)*span]
        blocks_in[c,s]=blocks_out[s]
        for index,(a,other) in enumerate(act_peers): act_copy(index,a,other).start()
    units=3*blocks
    ends=[sum(LAGS[:k+1]) for k in range(4)]
    last=ends[3]

    def pick(ref,slot,names,name,value):
        place=names.index(name)
        return ref.at[(slot,)+(slice(None),)*place+(value,)]
    def exchange(stage,kind,u):
        order=KINDS[kind]; name=order[stage]
        names=[n for n in NAMES if n not in order[:stage]]
        buffers=part if stage==0 else kept[stage-1][order is SHARD_FIRST]
        depth=buffers.shape[0]
        src=pick(buffers,lax.rem(u,depth),names,name,1-bit[name])
        target=came[stage][order is SHARD_FIRST]
        ring=lax.rem(u,target.shape[0])
        return pltpu.make_async_remote_copy(src_ref=src,dst_ref=target.at[ring],
            send_sem=send_sem[stage].at[ring],recv_sem=recv_sem[stage].at[ring],
            device_id=peer[name],device_id_type=MESH)
    def receive(stage,kind,u):
        order=KINDS[kind]; name=order[stage]
        names=[n for n in NAMES if n not in order[:stage]]
        exchange(stage,kind,u).wait()
        buffers=part if stage==0 else kept[stage-1][order is SHARD_FIRST]
        own=pick(buffers,lax.rem(u,buffers.shape[0]),names,name,bit[name])
        target=came[stage][order is SHARD_FIRST]
        other=target.at[lax.rem(u,target.shape[0])]
        left_over=len(names)-1
        if stage<3:
            result=kept[stage][order is SHARD_FIRST]
            slot=lax.rem(u,result.shape[0])
        for flat in range(1<<left_over):
            where=tuple((flat>>k)&1 for k in reversed(range(left_over)))
            total=own[where].astype(jnp.float32)+other[where].astype(jnp.float32)
            if stage<3: result[(slot,)+where]=total.astype(low)
            else: final[lax.rem(u,final.shape[0])]=total.astype(low)
        if stage<3: exchange(stage+1,kind,u).start()
    grad_qkv,grad_wout,grad_fc1,grad_fc2=outs
    anywhere=grad_fc2.at[0,0,:,:WIDTH]
    def placed(u,kind,action):
        block=u//3
        def columns(first): return pl.ds(pl.multiple_of((block-first)*D+kind*WIDTH,128),WIDTH)
        here=slice(kind*WIDTH,(kind+1)*WIDTH)
        pl.when(block<4)(lambda: action(lambda who: grad_fc2.at[block,who,:,here]))
        pl.when((block>=4)&(block<8))(lambda: action(lambda who: grad_fc1.at[who,:,columns(4)]))
        pl.when(block==8)(lambda: action(lambda who: grad_wout.at[who,:,here]))
        pl.when(block>=9)(lambda: action(lambda who: grad_qkv.at[who,:,columns(9)]))
    def spread(u,target):
        src=final.at[lax.rem(u,final.shape[0])]
        return (pltpu.make_async_copy(src,target,final_sem.at[u]),
            pltpu.make_async_remote_copy(src_ref=src,dst_ref=target,send_sem=far_send.at[u],recv_sem=far_recv.at[u],
                device_id=peer["r1"],device_id_type=MESH),
            pltpu.make_async_remote_copy(src_ref=src,dst_ref=target,send_sem=near_send.at[u],recv_sem=near_recv.at[u],
                device_id=peer["r0"],device_id_type=MESH))
    def relay(u,piece):
        return pltpu.make_async_remote_copy(src_ref=piece,dst_ref=piece,send_sem=fwd_send.at[u],recv_sem=fwd_recv.at[u],
                device_id=peer["r0"],device_id_type=MESH)
    def compute(kind,block,u):
        slot=lax.rem(block,2)
        columns=right[slot,:,kind*WIDTH:(kind+1)*WIDTH]
        rows=left.shape[2]//4
        for shard in range(4):
            product=lax.dot_general(left[slot,shard],columns,(((1,),(0,)),((),())),preferred_element_type=jnp.float32)
            for rep in range(4):
                part[lax.rem(u,part.shape[0]),shard//2,shard%2,rep//2,rep%2]=product[rep*rows:(rep+1)*rows].astype(low)
        exchange(0,kind,u).start()

    total_steps=units+last+4
    iterations=-(-total_steps//3)
    def iteration(it,carry):
        @pl.when(it<blocks)
        def _():
            slot=lax.rem(it,2)
            pltpu.make_async_copy(left.at[slot],left.at[slot],left_sem.at[slot]).wait()
            pltpu.make_async_copy(right.at[slot],right.at[slot],right_sem.at[slot]).wait()
        for sub in range(3):
            step=3*it+sub
            def at(lag,action):
                kind=(sub-lag)%3
                unit=step-lag
                @pl.when((unit>=0)&(unit<units))
                def _(): action(kind,unit)
            def finish(kind,u):
                local,far,near=spread(u,anywhere)
                local.wait(); far.wait_send(); near.wait(); relay(u,anywhere).wait()
            at(last+3,finish)
            def pass_on(kind,u):
                spread(u,anywhere)[1].wait_recv()
                placed(u,kind,lambda where: relay(u,where(across)).start())
            at(last+2,pass_on)
            def finalize(kind,u):
                receive(3,kind,u)
                def start(where):
                    for copy in spread(u,where(r)): copy.start()
                placed(u,kind,start)
            at(ends[3],finalize)
            for stage in (2,1,0):
                at(ends[stage],functools.partial(receive,stage))
            if sub==0:
                load(it+1,lax.rem(it+1,2))
                pl.when(it==3)(share_notes)
            at(0,lambda kind,u: compute(kind,it,u))
        return carry
    lax.fori_loop(0,iterations,iteration,0)
    for index,(a,other) in enumerate(act_peers): act_copy(index,a,other).wait()
    act_out[...]=blocks_in[0]+blocks_in[1]

def unpack(refs):
    refs=list(refs)
    left,right,left_sem,right_sem,part=refs[:5]; refs=refs[5:]
    came=[(refs[0],refs[0]),(refs[1],refs[2]),(refs[3],refs[4]),(refs[5],refs[5])]; refs=refs[6:]
    send=refs[:4]; recv=refs[4:8]; refs=refs[8:]
    kept=[(refs[0],refs[0]),(refs[1],refs[2]),(refs[3],refs[4])]; refs=refs[5:]
    return (left,right,left_sem,right_sem,part,came,send,recv,kept,*refs)

def reduce_all(halves,note,ada):
    shards=lax.axis_size("shard"); reps=lax.axis_size("rep")
    rows=D//(shards*reps); group=D//shards
    blocks=12; units=3*blocks
    operands=[]
    for pairs in halves:
        (hidden,feed),(second,pre),(att,branch),(first,project)=pairs
        span=hidden.shape[0]
        operands+=[a.T.reshape(shards,group,span) for a in (first,second,att)]
        operands+=[hidden.T.reshape(shards,4,group,span),feed,pre,branch,project]
    tokens=2*span
    any_=pl.BlockSpec(memory_space=pl.ANY)
    piece=(rows,WIDTH)
    two=lambda count: (2,)*count+piece
    rings=[2*lag+1 for lag in LAGS]
    vm=lambda depth,shape: pltpu.VMEM((depth,)+shape,low)
    dma=pltpu.SemaphoreType.DMA
    keep=[lag+1 for lag in LAGS]
    inside=pl.BlockSpec(memory_space=pltpu.VMEM)
    batch=note.shape[0]
    made=lambda shape,dtype: jax.ShapeDtypeStruct(shape,dtype)
    *grads,notes,act_grad=pl.pallas_call(functools.partial(reduce_kernel,blocks),
        in_specs=[any_]*16+[inside,any_],out_specs=[any_]*4+[inside,inside],
        out_shape=[made((reps,rows,3*D),low),made((reps,rows,D),low),made((reps,rows,4*D),low),made((4,reps,rows,D),low),
            made((shards*reps*batch,note.shape[1]),low),made((shards,batch,group),jnp.float32)],
        scratch_shapes=[
            pltpu.VMEM((2,shards,group,tokens),low),pltpu.VMEM((2,tokens,D),low),dma((2,)),dma((2,)),
            vm(keep[0],two(4)),
            vm(rings[0],two(3)),vm(rings[1],two(2)),vm(rings[1],two(2)),vm(rings[2],two(1)),vm(rings[2],two(1)),vm(rings[3],two(0)),
            *[dma((ring,)) for ring in rings],*[dma((ring,)) for ring in rings],
            vm(keep[1],two(3)),vm(keep[2],two(2)),vm(keep[2],two(2)),vm(keep[3],two(1)),vm(keep[3],two(1)),
            vm(5,piece),
            *[dma((units,)) for _ in range(7)],dma((15,)),dma((15,)),
            pltpu.VMEM((shards*reps,)+note.shape,low),pltpu.VMEM(ada.shape,low),dma(()),dma(()),
            pltpu.VMEM((shards,batch,group),jnp.float32),pltpu.VMEM((2,shards,batch,group),jnp.float32),dma((7,)),dma((7,))],
        compiler_params=pltpu.CompilerParams(collective_id=2,has_side_effects=True),
        cost_estimate=pl.CostEstimate(flops=2*tokens*D*D*blocks,bytes_accessed=4*tokens*D*blocks,transcendentals=0),
        )(*operands,note,ada)
    grads=[grad.reshape(-1,grad.shape[-1]).astype(jnp.float32) for grad in grads]
    return grads,notes,act_grad


def body(
    latents,
    cond,
    modulation_weight,
    query_key_value_weight,
    attention_output_weight,
    feed_first_weight,
    feed_second_weight,
    cotangent,
):
    first_section = lax.axis_index("section") == 0
    shard = lax.axis_index("shard")
    rep = lax.axis_index("rep")
    shards = lax.axis_size("shard")
    reps = lax.axis_size("rep")
    batch = latents.shape[0]
    modulation_weight = modulation_weight[0]
    rows = modulation_weight.shape[0]

    cond_float = cond.astype(jnp.float32)
    act = jax.nn.silu(cond_float).astype(low)
    came = exchange_shards(act.reshape(batch, shards, rows).transpose(1, 0, 2))
    partial = matmul(jnp.concatenate(came, axis=0), modulation_weight)
    partial = partial.reshape(shards, batch, -1)
    total = partial[0]
    for step in range(1, shards):
        total = total + lax.ppermute(
            partial[step], "shard", [(i, (i - step) % shards) for i in range(shards)]
        )
    def pick(section_zero, section_one):
        rows_of = jnp.where(
            first_section,
            total[section_zero : section_zero + 1],
            total[section_one : section_one + 1],
        )
        return jnp.split(rows_of[:, None, :], 6, axis=-1)

    weights = gather_all(
        (
            query_key_value_weight[0],
            attention_output_weight[0],
            feed_first_weight[0],
            feed_second_weight[0],
        )
    )

    forth = [(0, 1)]
    back = [(1, 0)]
    latent = (latents[:1], latents[1:])
    grad_out = (cotangent[:1], cotangent[1:])
    mod_zero, mod_one, mod_two = pick(0, 0), pick(1, 0), pick(0, 1)
    _, early, _ = forward_layer(latent[0].astype(jnp.float32), mod_zero, weights)
    incoming = lax.ppermute(early, "section", forth)
    input_one = jnp.where(first_section, latent[1], incoming).astype(jnp.float32)
    result_one, sent, kept_one = forward_layer(input_one, mod_one, weights)
    incoming = lax.ppermute(sent, "section", forth)
    early, _, _ = backward_layer(
        input_one, mod_one, weights, kept_one, grad_out[0].astype(jnp.float32)
    )
    early = early.astype(low)
    returning = lax.ppermute(early, "section", back)
    incoming, early = lax.optimization_barrier((incoming, early))
    input_two = jnp.where(first_section, latent[0], incoming).astype(jnp.float32)
    result_two, _, kept_two = forward_layer(input_two, mod_two, weights)
    grad_result = jnp.where(first_section, returning, grad_out[1]).astype(jnp.float32)
    grad_in_one, grad_mod_one, pairs_one = backward_layer(
        input_two, mod_two, weights, kept_two, grad_result
    )
    returning = lax.ppermute(grad_in_one.astype(low), "section", back)
    grad_result = jnp.where(first_section, returning, grad_out[0]).astype(jnp.float32)
    grad_in_two, grad_mod_two, pairs_two = backward_layer(
        input_one, mod_one, weights, kept_one, grad_result
    )
    grad_mod = jnp.where(
        first_section,
        jnp.concatenate([grad_mod_one, grad_mod_two], axis=0),
        jnp.concatenate([grad_mod_two, grad_mod_one], axis=0),
    )
    packed = jnp.concatenate([grad_mod, act], axis=-1)
    if shards == 4 and reps == 4:
        (grad_qkv, grad_wout, grad_fc1, grad_fc2), packed, act_grad = reduce_all(
            (pairs_one, pairs_two), packed, modulation_weight
        )
        act_total = act_grad.transpose(1, 0, 2).reshape(batch, shards * rows)
    else:
        pairs = [
            [jnp.concatenate(halves, axis=0) for halves in zip(one, two)]
            for one, two in zip(pairs_one, pairs_two)
        ]
        grad_fc2 = reduce_rows(*pairs[0], True)
        grad_fc1 = reduce_rows(*pairs[1], False)
        grad_wout = reduce_rows(*pairs[2], True)
        grad_qkv = reduce_rows(*pairs[3], True)
        packed = lax.all_gather(packed, ("shard", "rep"), axis=0, tiled=True)
        own_mod = lax.dynamic_index_in_dim(
            packed[:, : grad_mod.shape[1]].reshape(shards, reps, batch, -1), rep, 1, keepdims=False
        ).reshape(shards * batch, -1)
        act_grad = matmul_t(own_mod, modulation_weight)
        act_grad = act_grad + lax.ppermute(act_grad, "section", [(0, 1), (1, 0)])
        came = exchange_shards(act_grad.reshape(shards, batch, rows))
        act_total = jnp.zeros((shards, batch, rows), jnp.float32)
        for step, block in enumerate(came):
            act_total = lax.dynamic_update_index_in_dim(
                act_total, block, (shard - step) % shards, 0
            )
        act_total = act_total.transpose(1, 0, 2).reshape(batch, shards * rows)

    boundary = jnp.concatenate(
        [
            jnp.where(first_section, grad_in_one, result_one),
            jnp.where(first_section, grad_in_two, result_two),
        ],
        axis=0,
    )[None]

    all_mod = packed[:, : grad_mod.shape[1]]
    all_act = packed[:, grad_mod.shape[1] :]
    act_rows = lax.dynamic_slice_in_dim(all_act, shard * rows, rows, 1)
    grad_ada = lax.dot_general(
        act_rows, all_mod, (((0,), (0,)), ((), ())), preferred_element_type=jnp.float32
    )
    _, silu_back = jax.vjp(jax.nn.silu, cond_float)
    grad_cond = silu_back(act_total)[0]
    return (
        boundary,
        grad_cond,
        grad_ada[None],
        grad_qkv[None],
        grad_wout[None],
        grad_fc1[None],
        grad_fc2[None],
    )


def solution(mesh):
    in_specs = (
        P(("shard", "rep"), None, None),
        P(("shard", "rep"), None),
        P("section", "shard", None),
        P("section", "shard", None),
        P("section", "shard", None),
        P("section", "shard", None),
        P("section", "shard", None),
        P(("shard", "rep"), None, None),
    )
    out_specs = (
        P("section", ("shard", "rep"), None, None),
        P(("shard", "rep"), None),
        P("section", "shard", None),
        P("section", "shard", None),
        P("section", "shard", None),
        P("section", "shard", None),
        P("section", "shard", None),
    )

    return jax.shard_map(body, mesh=mesh, in_specs=in_specs, out_specs=out_specs, check_vma=False)
```

profile of v0, /device:TPU:0, one launch (start us, length us, event | category | flops | bytes accessed | tf_op | source)
XLA Modules:
  0.0 687.8 jit_solution(12996082876321904714)
XLA Ops:
  1.5 5.1 collective-permute-start.2
  12.1 2.8 fusion.91
  16.7 2.3 collective-permute-start.3
  19.0 158.5 %shard_map.135 = (bf16[4,4,72,3456]{3,2,1,0:T(8,128)(2,1)}, bf16[4,4,72,1152]{3,2,1,0:T(8,128)(2,1)}, bf16[4,4,72,4608]{3,2,1,0:T(8,128)(2,1)}, bf16[4,4,288,1152]{3,2,1,0:T(8,128)(2,1)}) custom-call(bf16[4,72,3456]{2,1,0:T(8,128)(2,1)} %bitcast.260, bf16[4,72,1152]{2,1,0:T(8,128)(2,1)} %bitcast.262, bf16[4,72,4608]{2,1,0:T(8,128)(2,1)} %bitcast.251, ...), custom_call_target="tpu_custom_call" | custom-call | tf_op jit(solution)/shard_map/pallas_call | solution.py:411
  178.2 7.5 %convolution_convert_fusion.2.project_ref = bf16[256,3456]{1,0:T(8,128)(2,1)} fusion(bf16[1152,3456]{1,0:T(8,128)(2,1)} %bitcast.274, f32[1152]{0:T(1024)S(1)} %get-tuple-element.89, f32[1152]{0:T(1024)S(1)} %get-tuple-element.90, f32[256]{0:T(256)S(1)} %add_rsqrt_fusion.5, f32[256]{0:T(256)S(1)} %broadcast_multiply_fusion.17, bf16[2,256,1152]{2,1,0:T(8,128)(2,1)} %param.8), kind=kOutput, calls=%fused_computation.3 | convolution fusion | flops 2041085952 | bytes 10333184 | tf_op jit(solution)/shard_map/dot_general | solution.py:152
  185.8 4.8 shard_map.136
  190.6 2.3 fusion.121
  194.3 15.5 %shard_map.137 = (f32[256,4608]{1,0:T(8,128)}, bf16[256,4608]{1,0:T(8,128)(2,1)}, f32[256,1152]{1,0:T(8,128)}, f32[256,1152]{1,0:T(8,128)}, bf16[256,1152]{1,0:T(8,128)(2,1)}) custom-call(bf16[256,1152]{1,0:T(8,128)(2,1)} %fusion.59.x_ref, f32[256,1152]{1,0:T(8,128)} %bitcast.241, f32[1,1152]{1,0:T(1,128)} %get-tuple-element.122.gate_ref, ...), custom_call_target="tpu_custom_call" | custom-call | flops 5435817984 | bytes 33030144 | tf_op jit(solution)/shard_map/pallas_call | solution.py:123
  209.8 3.7 collective-permute-start.6
  214.8 2.0 fusion.66.g_ref
  216.8 10.0 %collective-permute-done.6 = bf16[1,256,1152]{2,1,0:T(8,128)(2,1)S(1)} collective-permute-done((bf16[1,256,1152]{2,1,0:T(8,128)(2,1)}, bf16[1,256,1152]{2,1,0:T(8,128)(2,1)S(1)}, u32[]{:S(2)}, u32[]{:S(2)}) %collective-permute-start.6) | collective-permute-done | bytes 589856 | tf_op jit(solution)/shard_map/ppermute | solution.py:698
  227.4 7.2 %convolution_convert_fusion.1.project_ref = bf16[256,3456]{1,0:T(8,128)(2,1)} fusion(bf16[1152,3456]{1,0:T(8,128)(2,1)} %bitcast.275, bf16[1,256,1152]{2,1,0:T(8,128)(2,1)S(1)} %get-tuple-element.109, f32[1152]{0:T(1024)S(1)} %get-tuple-element.140, f32[1152]{0:T(1024)S(1)} %get-tuple-element.139, f32[256]{0:T(256)S(1)} %add_rsqrt_fusion.3, ...), kind=kOutput, calls=%fused_computation.2 | convolution fusion | flops 2041085952 | bytes 10333184 | tf_op jit(solution)/shard_map/dot_general | solution.py:152
  234.6 4.9 shard_map.138
  239.5 2.1 fusion.109
  244.6 15.5 %shard_map.139 = (f32[256,4608]{1,0:T(8,128)}, bf16[256,4608]{1,0:T(8,128)(2,1)}, f32[256,1152]{1,0:T(8,128)}, f32[256,1152]{1,0:T(8,128)}, bf16[256,1152]{1,0:T(8,128)(2,1)}) custom-call(bf16[256,1152]{1,0:T(8,128)(2,1)} %fusion.79.x_ref, f32[256,1152]{1,0:T(8,128)} %get-tuple-element.110.middle_ref, f32[1,1152]{1,0:T(1,128)} %get-tuple-element.136.gate_ref, ...), custom_call_target="tpu_custom_call" | custom-call | flops 5435817984 | bytes 33030144 | tf_op jit(solution)/shard_map/pallas_call | solution.py:123
  260.1 14.3 %shard_map.140 = (bf16[256,4608]{1,0:T(8,128)(2,1)}, f32[256,1152]{1,0:T(8,128)}) custom-call(bf16[256,1152]{1,0:T(8,128)(2,1)} %fusion.66.g_ref, bf16[1152,4608]{1,0:T(8,128)(2,1)} %bitcast.230, bf16[4608,1152]{1,0:T(8,128)(2,1)} %bitcast.236, f32[256,4608]{1,0:T(8,128)} %get-tuple-element.38.u_ref), custom_call_target="tpu_custom_call" | custom-call | flops 5435817984 | bytes 30081024 | tf_op jit(solution)/shard_map/pallas_call | solution.py:132
  277.4 5.3 collective-permute-start.8
  283.9 3.3 convolution_convert_fusion.5.grad_ref
  287.2 9.3 %shard_map.141 = bf16[256,3456]{1,0:T(8,128)(2,1)} custom-call(bf16[256,3456]{1,0:T(8,128)(2,1)} %convolution_convert_fusion.1.project_ref, bf16[256,1152]{1,0:T(8,128)(2,1)} %convolution_convert_fusion.5.grad_ref), custom_call_target="tpu_custom_call" | custom-call | flops 754974720 | bytes 4128768 | tf_op jit(solution)/shard_map/pallas_call | solution.py:68
  296.6 7.4 %fusion.28 = (f32[256]{0:T(256)S(1)}, f32[256,1152]{1,0:T(8,128)}) fusion(bf16[1,256,1152]{2,1,0:T(8,128)(2,1)S(1)} %get-tuple-element.109, f32[256]{0:T(256)S(1)} %copy-done.66, f32[256]{0:T(256)S(1)} %copy-done.59, f32[1152]{0:T(1024)S(1)} %copy-done.37, bf16[256,3456]{1,0:T(8,128)(2,1)} %shard_map.141, bf16[1152,3456]{1,0:T(8,128)(2,1)} %bitcast.276), kind=kOutput, calls=%fused_computation.56 | convolution fusion | flops 2040200960 | bytes 11509248 | tf_op jit(solution)/shard_map/dot_general | solution.py:156
  304.5 1.9 reduce_sum.331
  307.1 3.0 fusion.32
  310.1 1.8 collective-permute-start.7
  314.1 4.4 copy.35
  319.7 7.2 %convolution_convert_fusion.project_ref = bf16[256,3456]{1,0:T(8,128)(2,1)} fusion(bf16[1152,3456]{1,0:T(8,128)(2,1)} %bitcast.277, bf16[1,256,1152]{2,1,0:T(8,128)(2,1)S(1)} %get-tuple-element.107, f32[1152]{0:T(1024)S(1)} %copy-done.55, f32[1152]{0:T(1024)S(1)} %copy-done.39, f32[256]{0:T(256)S(1)} %add_rsqrt_fusion.1, f32[256]{0:T(256)S(1)} %broadcast_multiply_fusion.9), kind=kOutput, calls=%fused_computation.1 | convolution fusion | flops 2041085952 | bytes 10333184 | tf_op jit(solution)/shard_map/dot_general | solution.py:152
  326.9 4.8 shard_map.142
  331.7 4.0 fusion.119
  337.6 15.6 %shard_map.143 = (f32[256,4608]{1,0:T(8,128)}, bf16[256,4608]{1,0:T(8,128)(2,1)}, f32[256,1152]{1,0:T(8,128)}, f32[256,1152]{1,0:T(8,128)}, bf16[256,1152]{1,0:T(8,128)(2,1)}) custom-call(bf16[256,1152]{1,0:T(8,128)(2,1)} %fusion.143.x_ref, f32[256,1152]{1,0:T(8,128)} %bitcast.240, f32[1,1152]{1,0:T(1,128)} %get-tuple-element.120.gate_ref, ...), custom_call_target="tpu_custom_call" | custom-call | flops 5435817984 | bytes 33030144 | tf_op jit(solution)/shard_map/pallas_call | solution.py:123
  353.2 2.2 fusion.46
  356.4 14.4 %shard_map.144 = (bf16[256,4608]{1,0:T(8,128)(2,1)}, f32[256,1152]{1,0:T(8,128)}) custom-call(bf16[256,1152]{1,0:T(8,128)(2,1)} %fusion.65.g_ref.refs_4_, bf16[1152,4608]{1,0:T(8,128)(2,1)} %bitcast.232, bf16[4608,1152]{1,0:T(8,128)(2,1)} %bitcast.238, f32[256,4608]{1,0:T(8,128)} %get-tuple-element.42.u_ref), custom_call_target="tpu_custom_call" | custom-call | flops 5435817984 | bytes 30081024 | tf_op jit(solution)/shard_map/pallas_call | solution.py:132
  370.9 2.4 fusion.51
  378.0 1.9 convolution_convert_fusion.4.grad_ref
  379.9 9.3 %shard_map.145.refs_7_ = bf16[256,3456]{1,0:T(8,128)(2,1)} custom-call(bf16[256,3456]{1,0:T(8,128)(2,1)} %convolution_convert_fusion.project_ref, bf16[256,1152]{1,0:T(8,128)(2,1)} %convolution_convert_fusion.4.grad_ref), custom_call_target="tpu_custom_call" | custom-call | flops 754974720 | bytes 4128768 | tf_op jit(solution)/shard_map/pallas_call | solution.py:68
  389.2 7.1 %fusion.115 = (bf16[1152]{0:T(1024)(128)(2,1)}, f32[256]{0:T(256)S(1)}, f32[256,1152]{1,0:T(8,128)S(1)}) fusion(f32[1152]{0:T(1024)S(1)} %copy-done.40, bf16[256,3456]{1,0:T(8,128)(2,1)} %shard_map.145.refs_7_, bf16[1152,3456]{1,0:T(8,128)(2,1)} %bitcast.278), kind=kOutput, calls=%fused_computation.245 | convolution fusion | flops 2039315072 | bytes 10919680 | tf_op jit(solution)/shard_map/dot_general | solution.py:156
  397.9 1.9 bitcast_select_fusion
  404.7 4.4 copy.31
  409.2 9.1 %collective-permute-done.9 = bf16[1,256,1152]{2,1,0:T(8,128)(2,1)} collective-permute-done((bf16[1,256,1152]{2,1,0:T(8,128)(2,1)}, bf16[1,256,1152]{2,1,0:T(8,128)(2,1)}, u32[]{:S(2)}, u32[]{:S(2)}) %collective-permute-start.9) | collective-permute-done | bytes 589856 | tf_op jit(solution)/shard_map/ppermute | solution.py:714
  418.3 2.3 fusion.48
  421.5 14.2 %shard_map.146 = (bf16[256,4608]{1,0:T(8,128)(2,1)}, f32[256,1152]{1,0:T(8,128)}) custom-call(bf16[256,1152]{1,0:T(8,128)(2,1)} %fusion.64.g_ref.refs_12_, bf16[1152,4608]{1,0:T(8,128)(2,1)} %bitcast.233, bf16[4608,1152]{1,0:T(8,128)(2,1)} %bitcast.239, f32[256,4608]{1,0:T(8,128)} %get-tuple-element.38.u_ref), custom_call_target="tpu_custom_call" | custom-call | flops 5435817984 | bytes 30081024 | tf_op jit(solution)/shard_map/pallas_call | solution.py:132
  435.7 2.2 fusion.49
  441.0 1.9 convolution_convert_fusion.3.grad_ref
  442.9 9.3 %shard_map.147.refs_15_ = bf16[256,3456]{1,0:T(8,128)(2,1)} custom-call(bf16[256,3456]{1,0:T(8,128)(2,1)} %convolution_convert_fusion.1.project_ref, bf16[256,1152]{1,0:T(8,128)(2,1)} %convolution_convert_fusion.3.grad_ref), custom_call_target="tpu_custom_call" | custom-call | flops 754974720 | bytes 4128768 | tf_op jit(solution)/shard_map/pallas_call | solution.py:68
  452.2 7.1 %fusion.117 = (bf16[1152]{0:T(1024)(128)(2,1)}, f32[256]{0:T(256)S(1)}, f32[256,1152]{1,0:T(8,128)S(1)}) fusion(f32[1152]{0:T(1024)S(1)} %copy-done.38, bf16[256,3456]{1,0:T(8,128)(2,1)} %shard_map.147.refs_15_, bf16[1152,3456]{1,0:T(8,128)(2,1)} %bitcast.279), kind=kOutput, calls=%fused_computation.247 | convolution fusion | flops 2039315072 | bytes 10919680 | tf_op jit(solution)/shard_map/dot_general | solution.py:156
  468.3 198.5 %shard_map.148 = (bf16[4,72,3456]{2,1,0:T(8,128)(2,1)}, bf16[4,72,1152]{2,1,0:T(8,128)(2,1)}, bf16[4,72,4608]{2,1,0:T(8,128)(2,1)}, bf16[4,4,72,1152]{3,2,1,0:T(...) custom-call(bf16[4,288,256]{2,1,0:T(8,128)(2,1)} %bitcast.265, bf16[4,288,256]{2,1,0:T(8,128)(2,1)} %bitcast.266, ...), custom_call_target="tpu_custom_call" | custom-call | flops 16307453952 | bytes 28311552 | tf_op jit(solution)/shard_map/pallas_call | solution.py:625
  669.1 3.9 bitcast_convert_fusion.1
  674.1 3.0 bitcast_convert_fusion
  677.2 2.7 convert.67
  682.8 4.5 convolution_bitcast_fusion
  (274 shorter events, 57.1 us)
Async XLA Ops:
  1.4 10.7 %copy-start.48 = (bf16[2,1152]{1,0:T(2,128)(2,1)}, bf16[2,1152]{1,0:T(2,128)(2,1)S(1)}, u32[]{:S(2)}) copy-start(bf16[2,1152]{1,0:T(2,128)(2,1)S(1)} %fusion.88) | copy-start | bytes 13828
  1.5 8.8 %collective-permute-start.2 = (bf16[2,288]{1,0:T(2,128)(2,1)S(1)}, bf16[2,288]{1,0:T(2,128)(2,1)S(1)}, u32[]{:S(2)}, u32[]{:S(2)}) collective-permute-start(bf16[2,288]{1,0:T(2,128)(2,1)S(1)} %bitcast.271), channel_id=1, source_target_pairs={{0,12},{4,0},{8,4},{12,8},{1,13},{5,1},{9,5},{13,9},{2,14},{6,2},{... | collective-permute-start | bytes 3464 | tf_op jit(solution)/shard_map/ppermute | solution.py:312
  6.7 4.5 collective-permute-start.1
  6.7 5.4 collective-permute-start
  15.0 162.5 %collective-permute-start.5 = (f32[2,6912]{1,0:T(2,128)S(1)}, f32[2,6912]{1,0:T(2,128)S(1)}, u32[]{:S(2)}, u32[]{:S(2)}) collective-permute-start(f32[2,6912]{1,0:T(2,128)S(1)} %get-tuple-element.115), channel_id=1, source_target_pairs={{0,4},{4,8},{8,12},{12,0},{1,5},{5,9},{9,13},{13,1},{2,6},{6,10},{... | collective-permute-start | bytes 165896 | tf_op jit(solution)/shard_map/ppermute | solution.py:672
  15.7 161.8 %collective-permute-start.4 = (f32[2,6912]{1,0:T(2,128)S(1)}, f32[2,6912]{1,0:T(2,128)S(1)}, u32[]{:S(2)}, u32[]{:S(2)}) collective-permute-start(f32[2,6912]{1,0:T(2,128)S(1)} %get-tuple-element.116), channel_id=1, source_target_pairs={{0,8},{4,12},{8,0},{12,4},{1,9},{5,13},{9,1},{13,5},{2,10},{6,14},... | collective-permute-start | bytes 165896 | tf_op jit(solution)/shard_map/ppermute | solution.py:672
  16.7 160.8 %collective-permute-start.3 = (f32[2,6912]{1,0:T(2,128)S(1)}, f32[2,6912]{1,0:T(2,128)S(1)}, u32[]{:S(2)}, u32[]{:S(2)}) collective-permute-start(f32[2,6912]{1,0:T(2,128)S(1)} %get-tuple-element.114), channel_id=1, source_target_pairs={{0,12},{4,0},{8,4},{12,8},{1,13},{5,1},{9,5},{13,9},{2,14},{6,2},{... | collective-permute-start | bytes 165896 | tf_op jit(solution)/shard_map/ppermute | solution.py:672
  178.2 12.4 %copy-start.5 = (bf16[4,4,72,1152]{3,2,1,0:T(8,128)(2,1)S(1)}, bf16[4,4,72,1152]{3,2,1,0:T(8,128)(2,1)}, u32[]{:S(2)}) copy-start(bf16[4,4,72,1152]{3,2,1,0:T(8,128)(2,1)} %get-tuple-element.36) | copy-start | bytes 7962628
  209.8 17.0 %copy-start.21 = (bf16[2,256,1152]{2,1,0:T(8,128)(2,1)S(1)}, bf16[2,256,1152]{2,1,0:T(8,128)(2,1)}, u32[]{:S(2)}) copy-start(bf16[2,256,1152]{2,1,0:T(8,128)(2,1)} %param.8) | copy-start | bytes 3538948
  209.8 17.0 %collective-permute-start.6 = (bf16[1,256,1152]{2,1,0:T(8,128)(2,1)}, bf16[1,256,1152]{2,1,0:T(8,128)(2,1)S(1)}, u32[]{:S(2)}, u32[]{:S(2)}) collective-permute-start(bf16[1,256,1152]{2,1,0:T(8,128)(2,1)} %bitcast.280), channel_id=1, source_target_pairs={{0,16},{1,17},{2,18},{3,19},{4,20},{5,21},{6,22},{7,23},{8,24},{9,... | collective-permute-start | bytes 1769480 | tf_op jit(solution)/shard_map/ppermute | solution.py:698
  214.8 12.2 %copy-start.43 = (f32[1152]{0:T(1024)}, f32[1152]{0:T(1024)S(1)}, u32[]{:S(2)}) copy-start(f32[1152]{0:T(1024)S(1)} %get-tuple-element.137) | copy-start | bytes 13828
  214.8 12.6 %copy-start.36 = (f32[1152]{0:T(1024)}, f32[1152]{0:T(1024)S(1)}, u32[]{:S(2)}) copy-start(f32[1152]{0:T(1024)S(1)} %get-tuple-element.139) | copy-start | bytes 13828
  214.8 12.6 %copy-start.53 = (f32[1152]{0:T(1024)}, f32[1152]{0:T(1024)S(1)}, u32[]{:S(2)}) copy-start(f32[1152]{0:T(1024)S(1)} %get-tuple-element.140) | copy-start | bytes 13828
  227.1 7.6 %copy-start.58 = (f32[256]{0:T(256)}, f32[256]{0:T(256)S(1)}, u32[]{:S(2)}) copy-start(f32[256]{0:T(256)S(1)} %broadcast_multiply_fusion.15) | copy-start | bytes 3076
  227.4 7.3 %copy-start.65 = (f32[256]{0:T(256)}, f32[256]{0:T(256)S(1)}, u32[]{:S(2)}) copy-start(f32[256]{0:T(256)S(1)} %add_rsqrt_fusion.3) | copy-start | bytes 3076
  260.1 23.9 %copy-start.18 = (bf16[2,256,1152]{2,1,0:T(8,128)(2,1)S(1)}, bf16[2,256,1152]{2,1,0:T(8,128)(2,1)}, u32[]{:S(2)}) copy-start(bf16[2,256,1152]{2,1,0:T(8,128)(2,1)} %param.15) | copy-start | bytes 3538948
  274.4 9.6 %copy-start.6 = (bf16[4,4,72,1152]{3,2,1,0:T(8,128)(2,1)S(1)}, bf16[4,4,72,1152]{3,2,1,0:T(8,128)(2,1)}, u32[]{:S(2)}) copy-start(bf16[4,4,72,1152]{3,2,1,0:T(8,128)(2,1)} %get-tuple-element.36) | copy-start | bytes 7962628
  276.0 8.0 %copy-start.70 = (f32[256]{0:T(256)S(1)}, f32[256]{0:T(256)}, u32[]{:S(2)}) copy-start(f32[256]{0:T(256)} %copy-done.69) | copy-start | bytes 3076
  277.4 41.1 %collective-permute-start.8 = (bf16[1,256,1152]{2,1,0:T(8,128)(2,1)}, bf16[1,256,1152]{2,1,0:T(8,128)(2,1)}, u32[]{:S(2)}, u32[]{:S(2)}) collective-permute-start(bf16[1,256,1152]{2,1,0:T(8,128)(2,1)} %bitcast.34), channel_id=1, source_target_pairs={{0,16},{1,17},{2,18},{3,19},{4,20},{5,21},{6,22},{7,23},{8,24},{9,... | collective-permute-start | bytes 1769480 | tf_op jit(solution)/shard_map/ppermute | solution.py:701
  287.2 9.3 %copy-start.37 = (f32[1152]{0:T(1024)S(1)}, f32[1152]{0:T(1024)}, u32[]{:S(2)}) copy-start(f32[1152]{0:T(1024)} %copy-done.36) | copy-start | bytes 13828
  287.2 9.3 %copy-start.59 = (f32[256]{0:T(256)S(1)}, f32[256]{0:T(256)}, u32[]{:S(2)}) copy-start(f32[256]{0:T(256)} %copy-done.58) | copy-start | bytes 3076
  287.2 9.3 %copy-start.66 = (f32[256]{0:T(256)S(1)}, f32[256]{0:T(256)}, u32[]{:S(2)}) copy-start(f32[256]{0:T(256)} %copy-done.65) | copy-start | bytes 3076
  310.1 43.1 %collective-permute-start.7 = (bf16[1,256,1152]{2,1,0:T(8,128)(2,1)}, bf16[1,256,1152]{2,1,0:T(8,128)(2,1)}, u32[]{:S(2)}, u32[]{:S(2)}) collective-permute-start(bf16[1,256,1152]{2,1,0:T(8,128)(2,1)} %fusion.32), channel_id=1, source_target_pairs={{16,0},{17,1},{18,2},{19,3},{20,4},{21,5},{22,6},{23,7},{24,8},{25... | collective-permute-start | bytes 1769480 | tf_op jit(solution)/shard_map/ppermute | solution.py:706
  314.1 4.4 copy-start.22
  326.9 4.8 copy-start.41
  337.6 15.6 %copy-start.19 = (bf16[2,256,1152]{2,1,0:T(8,128)(2,1)S(1)}, bf16[2,256,1152]{2,1,0:T(8,128)(2,1)}, u32[]{:S(2)}) copy-start(bf16[2,256,1152]{2,1,0:T(8,128)(2,1)} %param.15) | copy-start | bytes 3538948
  356.4 14.4 %copy-start.1 = (f32[1,256,1152]{2,1,0:T(8,128)S(1)}, f32[1,256,1152]{2,1,0:T(8,128)}, u32[]{:S(2)}) copy-start(f32[1,256,1152]{2,1,0:T(8,128)} %copy-done) | copy-start | bytes 3538948
  379.9 9.3 %copy-start.40 = (f32[1152]{0:T(1024)S(1)}, f32[1152]{0:T(1024)}, u32[]{:S(2)}) copy-start(f32[1152]{0:T(1024)} %get-tuple-element.78) | copy-start | bytes 13828
  389.2 7.1 %copy-start.56 = (f32[1152]{0:T(1024)S(1)}, f32[1152]{0:T(1024)}, u32[]{:S(2)}) copy-start(f32[1152]{0:T(1024)} %get-tuple-element.77) | copy-start | bytes 13828
  389.2 7.1 %copy-start.77 = (f32[256]{0:T(256)S(1)}, f32[256]{0:T(256)}, u32[]{:S(2)}) copy-start(f32[256]{0:T(256)} %copy-done.76) | copy-start | bytes 3076
  389.2 7.1 %copy-start.80 = (f32[256]{0:T(256)S(1)}, f32[256]{0:T(256)}, u32[]{:S(2)}) copy-start(f32[256]{0:T(256)} %copy-done.79) | copy-start | bytes 3076
  399.8 18.5 %collective-permute-start.9 = (bf16[1,256,1152]{2,1,0:T(8,128)(2,1)}, bf16[1,256,1152]{2,1,0:T(8,128)(2,1)}, u32[]{:S(2)}, u32[]{:S(2)}) collective-permute-start(bf16[1,256,1152]{2,1,0:T(8,128)(2,1)} %get-tuple-element.103), channel_id=1, source_target_pairs={{16,0},{17,1},{18,2},{19,3},{20,4},{21,5},{22,6},{23,7},{24,8},{25... | collective-permute-start | bytes 1769480 | tf_op jit(solution)/shard_map/ppermute | solution.py:714
  404.7 4.4 copy-start.85
  404.7 4.4 copy-start.75
  404.7 4.4 copy-start.78
  404.7 4.5 copy-start.74
  404.7 4.5 copy-start.73
  404.7 4.5 copy-start.72
  404.7 13.6 %copy-start.20 = (bf16[2,256,1152]{2,1,0:T(8,128)(2,1)S(1)}, bf16[2,256,1152]{2,1,0:T(8,128)(2,1)}, u32[]{:S(2)}) copy-start(bf16[2,256,1152]{2,1,0:T(8,128)(2,1)} %param.15) | copy-start | bytes 3538948
  409.2 9.1 %copy-start.50 = (bf16[1,6912]{1,0:T(2,128)(2,1)}, bf16[1,6912]{1,0:T(2,128)(2,1)S(1)}, u32[]{:S(2)}) copy-start(bf16[1,6912]{1,0:T(2,128)(2,1)S(1)} %constant_dynamic-update-slice_fusion) | copy-start | bytes 41476
  442.9 9.3 %copy-start.38 = (f32[1152]{0:T(1024)S(1)}, f32[1152]{0:T(1024)}, u32[]{:S(2)}) copy-start(f32[1152]{0:T(1024)} %copy-done.36) | copy-start | bytes 13828
  452.2 7.1 %copy-start.54 = (f32[1152]{0:T(1024)S(1)}, f32[1152]{0:T(1024)}, u32[]{:S(2)}) copy-start(f32[1152]{0:T(1024)} %copy-done.53) | copy-start | bytes 13828
  452.2 7.1 %copy-start.60 = (f32[256]{0:T(256)S(1)}, f32[256]{0:T(256)}, u32[]{:S(2)}) copy-start(f32[256]{0:T(256)} %copy-done.58) | copy-start | bytes 3076
  452.2 7.1 %copy-start.67 = (f32[256]{0:T(256)S(1)}, f32[256]{0:T(256)}, u32[]{:S(2)}) copy-start(f32[256]{0:T(256)} %copy-done.65) | copy-start | bytes 3076
  460.4 7.2 %copy-start.49 = (bf16[2,1152]{1,0:T(2,128)(2,1)S(1)}, bf16[2,1152]{1,0:T(2,128)(2,1)}, u32[]{:S(2)}) copy-start(bf16[2,1152]{1,0:T(2,128)(2,1)} %copy-done.48) | copy-start | bytes 13828
  468.2 199.3 %copy-start.64 = (bf16[2,1152]{1,0:T(2,128)(2,1)S(1)}, bf16[2,1152]{1,0:T(2,128)(2,1)}, u32[]{:S(2)}) copy-start(bf16[2,1152]{1,0:T(2,128)(2,1)} %param.9) | copy-start | bytes 13828
  669.1 3.9 copy-start.30
  669.1 5.1 copy-start.26
  (48 other events, 80.9 us)
where the time goes:
time: 698 us; the launch traced here: 688 us
  Pallas kernels  489 us (70%)
  matrix products  66.3 us (9%)
  other arithmetic  59.2 us (8%)
  local copies, waits for them, and re-layouts  27.9 us (4%)
  starting transfers between devices  22.7 us (3%)
  waiting for transfers between devices  20.9 us (3%)
    pallas_call x1, Pallas kernels, reduce_all(): pl.pallas_call(functools.partial(reduce_kernel, blocks), in_specs=[any_]...  198 us
    pallas_call x1, Pallas kernels, gather_all(): pl.pallas_call(functools.partial(gather_kernel, shards, reps, count), in_...  158 us
    pallas_call x3, Pallas kernels, mlp(): pl.pallas_call(functools.partial(mlp_kernel, chunk), grid=(ff // tile,),...  46.5 us
    pallas_call x3, Pallas kernels, mlp_back(): pl.pallas_call(functools.partial(mlp_back_kernel, chunk), grid=(ff // til...  42.9 us
    dot_general x7, matrix products, matmul(): return jnp.dot(left, right, preferred_element_type=jnp.float32)  33.2 us
    dot_general x6, matrix products, matmul_t(): lax.dot_general(left, right, (((1,), (1,)), ((), ())), preferred_element_...  28.6 us
    pallas_call x3, Pallas kernels, attention_back(): pl.pallas_call(attention_back_kernel, grid=(tokens // length,), in_specs=...  27.9 us
    pallas_call x3, Pallas kernels, attention(): pl.pallas_call(attention_kernel, grid=(tokens // length,), in_specs=[pl.B...  14.5 us
  transfers between devices with their start and end apart: 10, of which 4 were waited for; matrix products, arithmetic and copies ran while one was open for 7% of the time, Pallas kernels for 27%

commit v1 on v0

--- a/solution.py
+++ b/solution.py
@@ -14,7 +14,6 @@
 LANES = 128
 
 
-epsilon = 1e-06
 low = jnp.bfloat16
 
 
@@ -57,95 +56,178 @@
         for base,piece in ((0,dq),(D,dk),(2*D,dv)):
             here=slice(base+first,base+last)
             out_ref[:,here]=jnp.where(mask,piece,out_ref[:,here])
-def attention(project,length):
-    tokens=project.shape[0]
-    return pl.pallas_call(attention_kernel,grid=(tokens//length,),
-        in_specs=[pl.BlockSpec((length,3*D),lambda i:(i,0))],out_specs=pl.BlockSpec((length,D),lambda i:(i,0)),
-        out_shape=jax.ShapeDtypeStruct((tokens,D),low),
-        cost_estimate=pl.CostEstimate(flops=4*tokens*length*D,bytes_accessed=8*tokens*D,transcendentals=HEADS*tokens*length))(project)
-def attention_back(project,grad,length):
-    tokens=project.shape[0]
-    return pl.pallas_call(attention_back_kernel,grid=(tokens//length,),
-        in_specs=[pl.BlockSpec((length,3*D),lambda i:(i,0)),pl.BlockSpec((length,D),lambda i:(i,0))],out_specs=pl.BlockSpec((length,3*D),lambda i:(i,0)),
-        out_shape=jax.ShapeDtypeStruct((tokens,3*D),low),
-        cost_estimate=pl.CostEstimate(flops=10*tokens*length*D,bytes_accessed=14*tokens*D,transcendentals=HEADS*tokens*length))(project,grad)
-
 C0=0.7978845608028654; C1=0.044715
+epsilon=1e-06
+FEED_GROUPS=3
+FEED_CHUNK=512
+
 def act_of(u): return (0.5*u*(1.0+jnp.tanh(C0*(u+C1*(u*u*u))))).astype(low)
 def slope_of(u):
     sq=u*u
     t=jnp.tanh(C0*(u+C1*(sq*u)))
     return 0.5*(1.0+t)+0.5*u*(1.0-t*t)*(C0*(1.0+3.0*C1*sq))
-def mlp_kernel(chunk,x_ref,middle_ref,gate_ref,w1_ref,w2_ref,u_ref,h_ref,f_ref,y_ref,y_low_ref):
-    tile=w1_ref.shape[1]
-    parts=[slice(a,a+chunk) for a in range(0,tile,chunk)]
-    first=pl.program_id(0)==0
-    @pl.when(first)
-    def _(): f_ref[...]=jnp.zeros_like(f_ref)
-    def front(p):
-        u=dot(x_ref[...],w1_ref[:,p]); u_ref[:,p]=u
-        return u
-    def back(p,u):
-        h=act_of(u); h_ref[:,p]=h
-        f_ref[...]+=dot(h,w2_ref[p,:])
-    prev=None
-    for p in parts:
-        u=front(p)
-        if prev is not None: back(*prev)
-        prev=(p,u)
-    back(*prev)
-    @pl.when(pl.program_id(0)==pl.num_programs(0)-1)
-    def _():
-        y=middle_ref[...]+gate_ref[...]*f_ref[...]
-        y_ref[...]=y
-        y_low_ref[...]=y.astype(low)
-def mlp_back_kernel(chunk,g_ref,w1_ref,w2_ref,u_ref,du_ref,dx_ref):
-    tile=w1_ref.shape[1]
-    parts=[slice(a,a+chunk) for a in range(0,tile,chunk)]
-    first=pl.program_id(0)==0
-    @pl.when(first)
-    def _(): dx_ref[...]=jnp.zeros_like(dx_ref)
-    def front(p): return dot(g_ref[...],w2_ref[p,:],NT)
-    def mid(p,dh):
-        du=(dh*slope_of(u_ref[:,p])).astype(low); du_ref[:,p]=du
-        return du
-    prev=None
-    for p in parts:
-        dh=front(p)
-        if prev is not None: dx_ref[...]+=dot(mid(*prev),w1_ref[:,prev[0]],NT)
-        prev=(p,dh)
-    dx_ref[...]+=dot(mid(*prev),w1_ref[:,prev[0]],NT)
-def mlp(x,middle,gate,w1,w2,tile=1536,chunk=512):
-    t,d=x.shape; ff=w1.shape[1]
-    whole=pl.BlockSpec((t,d),lambda i:(0,0))
-    cols=pl.BlockSpec((t,tile),lambda i:(0,i))
+def center_scale(values):
+    center=values-jnp.mean(values,axis=-1,keepdims=True)
+    scale=lax.rsqrt(jnp.mean(center*center,axis=-1,keepdims=True)+epsilon)
+    return center*scale,scale
+def norm_back(normed,scale,grad):
+    mean_grad=jnp.mean(grad,axis=-1,keepdims=True)
+    mean_dot=jnp.mean(grad*normed,axis=-1,keepdims=True)
+    return (grad-mean_grad-normed*mean_dot)*scale
+def chunks_of(span): return [slice(a,a+FEED_CHUNK) for a in range(0,span,FEED_CHUNK)]
+
+class Copies:
+    def __init__(self,sems): self.sems=sems; self.made=[]
+    def start(self,src,dst):
+        copy=pltpu.make_async_copy(src,dst,self.sems.at[len(self.made)])
+        copy.start(); self.made.append(copy)
+        return copy
+    def wait_all(self):
+        for copy in self.made: copy.wait()
+
+def forward_kernel(x_ref,mod_ref,wqkv,wout,w1,w2,
+        first_out,project_out,att_out,branch_out,middle_out,second_out,u_out,h_out,f_out,y_out,y_low_out,
+        wqkv_v,wout_v,w1_v,w2_v,first_v,project_v,att_v,branch_v,middle_v,second_v,u_v,h_v,f_v,y_v,y_low_v,in_sems,out_sems):
+    width=wqkv_v.shape[2]; group=w1_v.shape[2]
+    come=Copies(in_sems); leave=Copies(out_sems)
+    project_in=[come.start(wqkv.at[:,i*width:(i+1)*width],wqkv_v.at[i]) for i in range(3)]
+    out_in=come.start(wout,wout_v)
+    feed_in=[(come.start(w1.at[:,i*group:(i+1)*group],w1_v.at[i]),come.start(w2.at[i*group:(i+1)*group],w2_v.at[i])) for i in range(FEED_GROUPS)]
+    shift_one,scale_one,gate_one,shift_two,scale_two,gate_two=(mod_ref[:,i*D:(i+1)*D] for i in range(6))
+    x=x_ref[...].astype(jnp.float32)
+    first_v[...]=(center_scale(x)[0]*(1.0+scale_one)+shift_one).astype(low)
+    leave.start(first_v,first_out)
+    for i in range(3):
+        project_in[i].wait()
+        project_v[:,i*width:(i+1)*width]=dot(first_v[...],wqkv_v[i]).astype(low)
+    leave.start(project_v,project_out)
+    attention_kernel(project_v,att_v)
+    leave.start(att_v,att_out)
+    out_in.wait()
+    branch=dot(att_v[...],wout_v[...])
+    branch_v[...]=branch
+    leave.start(branch_v,branch_out)
+    middle=x_ref[...].astype(jnp.float32)+gate_one*branch
+    middle_v[...]=middle
+    leave.start(middle_v,middle_out)
+    second_v[...]=(center_scale(middle)[0]*(1.0+scale_two)+shift_two).astype(low)
+    leave.start(second_v,second_out)
+    for i in range(FEED_GROUPS):
+        for copy in feed_in[i]: copy.wait()
+        prev=None
+        def back(p,u):
+            h=act_of(u); h_v[i,:,p]=h
+            part=dot(h,w2_v[i,p,:])
+            if i==0 and p.start==0: f_v[...]=part
+            else: f_v[...]+=part
+        for p in chunks_of(group):
+            u=dot(second_v[...],w1_v[i,:,p]); u_v[i,:,p]=u
+            if prev is not None: back(*prev)
+            prev=(p,u)
+        back(*prev)
+        leave.start(u_v.at[i],u_out.at[:,i*group:(i+1)*group])
+        leave.start(h_v.at[i],h_out.at[:,i*group:(i+1)*group])
+    y=middle_v[...]+gate_two*f_v[...]
+    y_v[...]=y
+    y_low_v[...]=y.astype(low)
+    leave.start(y_low_v,y_low_out)
+    leave.start(f_v,f_out)
+    leave.start(y_v,y_out)
+    leave.wait_all()
+
+def backward_kernel(g_ref,mod_ref,x_ref,feed_out,middle,branch,u,project,wqkv,wout,w1,w2,
+        mod_out,df_out,du_out,do_out,dproject_out,dx_out,dx_low_out,
+        feed_v,middle_v,branch_v,u_v,project_v,wqkv_v,wout_v,w1_v,w2_v,df_v,du_v,do_v,datt_v,dproject_v,acc_v,dx_v,dx_low_v,in_sems,out_sems):
+    group=w1_v.shape[2]
+    come=Copies(in_sems); leave=Copies(out_sems)
+    feed_in=[]
+    for i in range(FEED_GROUPS):
+        feed_in.append((come.start(w2.at[i*group:(i+1)*group],w2_v.at[i]),come.start(u.at[:,i*group:(i+1)*group],u_v.at[i]),
+            come.start(w1.at[:,i*group:(i+1)*group],w1_v.at[i])))
+        if i==0: feed_copy=come.start(feed_out,feed_v)
+    middle_in=come.start(middle,middle_v); branch_in=come.start(branch,branch_v)
+    out_in=come.start(wout,wout_v); project_in=come.start(project,project_v); qkv_in=come.start(wqkv,wqkv_v)
+    _,scale_one,gate_one,_,scale_two,gate_two=(mod_ref[:,i*D:(i+1)*D] for i in range(6))
+    total=lambda values: jnp.sum(values,axis=0,keepdims=True)
+    df_v[...]=(gate_two*g_ref[...].astype(jnp.float32)).astype(low)
+    leave.start(df_v,df_out)
+    for i in range(FEED_GROUPS):
+        for copy in feed_in[i]: copy.wait()
+        prev=None
+        def back(p,dh):
+            du=(dh*slope_of(u_v[i,:,p])).astype(low); du_v[i,:,p]=du
+            part=dot(du,w1_v[i,:,p],NT)
+            if i==0 and p.start==0: acc_v[...]=part
+            else: acc_v[...]+=part
+        for p in chunks_of(group):
+            dh=dot(df_v[...],w2_v[i,p,:],NT)
+            if prev is not None: back(*prev)
+            prev=(p,dh)
+        back(*prev)
+        leave.start(du_v.at[i],du_out.at[:,i*group:(i+1)*group])
+    feed_copy.wait(); middle_in.wait(); branch_in.wait()
+    g=g_ref[...].astype(jnp.float32)
+    mod_out[:,5*D:6*D]=total(g*feed_v[...])
+    dh=acc_v[...]
+    normed,inverse=center_scale(middle_v[...])
+    mod_out[:,3*D:4*D]=total(dh)
+    mod_out[:,4*D:5*D]=total(dh*normed)
+    dmiddle=g+norm_back(normed,inverse,dh*(1.0+scale_two))
+    dx_v[...]=dmiddle
+    mod_out[:,2*D:3*D]=total(dmiddle*branch_v[...])
+    do_v[...]=(gate_one*dmiddle).astype(low)
+    leave.start(do_v,do_out)
+    out_in.wait()
+    datt_v[...]=dot(do_v[...],wout_v[...],NT).astype(low)
+    project_in.wait()
+    attention_back_kernel(project_v,datt_v,dproject_v)
+    leave.start(dproject_v,dproject_out)
+    qkv_in.wait()
+    dh=dot(dproject_v[...],wqkv_v[...],NT)
+    normed,inverse=center_scale(x_ref[...].astype(jnp.float32))
+    mod_out[:,0*D:1*D]=total(dh)
+    mod_out[:,1*D:2*D]=total(dh*normed)
+    dx=dx_v[...]+norm_back(normed,inverse,dh*(1.0+scale_one))
+    dx_v[...]=dx
+    dx_low_v[...]=dx.astype(low)
+    leave.start(dx_low_v,dx_low_out)
+    leave.start(dx_v,dx_out)
+    leave.wait_all()
+
+LAYER_VMEM=60 * 1024 * 1024
+def forward_layer(x,mod,weights):
+    _,_,w1,_=weights
+    t,d=x.shape; ff=w1.shape[1]; group=ff//FEED_GROUPS
     made=lambda width,dtype: jax.ShapeDtypeStruct((t,width),dtype)
-    return pl.pallas_call(functools.partial(mlp_kernel,chunk),grid=(ff//tile,),
-        in_specs=[whole,whole,pl.BlockSpec((1,d),lambda i:(0,0)),pl.BlockSpec((d,tile),lambda i:(0,i)),pl.BlockSpec((tile,d),lambda i:(i,0))],
-        out_specs=[cols,cols,whole,whole,whole],
-        out_shape=[made(ff,jnp.float32),made(ff,low),made(d,jnp.float32),made(d,jnp.float32),made(d,low)],
-        cost_estimate=pl.CostEstimate(flops=4*t*d*ff,bytes_accessed=4*d*ff+6*t*ff+16*t*d,transcendentals=t*ff))(x,middle,gate,w1,w2)
-def mlp_back(g,w1,w2,u,tile=1536,chunk=512):
-    t,d=g.shape; ff=w1.shape[1]
-    whole=pl.BlockSpec((t,d),lambda i:(0,0))
-    cols=pl.BlockSpec((t,tile),lambda i:(0,i))
-    return pl.pallas_call(functools.partial(mlp_back_kernel,chunk),grid=(ff//tile,),
-        in_specs=[whole,pl.BlockSpec((d,tile),lambda i:(0,i)),pl.BlockSpec((tile,d),lambda i:(i,0)),cols],
-        out_specs=[cols,whole],
-        out_shape=[jax.ShapeDtypeStruct((t,ff),low),jax.ShapeDtypeStruct((t,d),jnp.float32)],
-        cost_estimate=pl.CostEstimate(flops=4*t*d*ff,bytes_accessed=4*d*ff+6*t*ff+6*t*d,transcendentals=t*ff))(g,w1,w2,u)
-
-
-def center_scale(values):
-    center = values - jnp.mean(values, axis=-1, keepdims=True)
-    scale = lax.rsqrt(jnp.mean(center * center, axis=-1, keepdims=True) + epsilon)
-    return center * scale, scale
-
-
-def norm_back(normed, scale, grad):
-    mean_grad = jnp.mean(grad, axis=-1, keepdims=True)
-    mean_dot = jnp.mean(grad * normed, axis=-1, keepdims=True)
-    return (grad - mean_grad - normed * mean_dot) * scale
+    f32=jnp.float32
+    v=pltpu.VMEM
+    any_=pl.BlockSpec(memory_space=pl.ANY); inside=pl.BlockSpec(memory_space=pltpu.VMEM)
+    return pl.pallas_call(forward_kernel,in_specs=[inside,inside]+[any_]*4,out_specs=[any_]*11,
+        out_shape=[made(d,low),made(3*d,low),made(d,low),made(d,f32),made(d,f32),made(d,low),made(ff,f32),made(ff,low),made(d,f32),made(d,f32),made(d,low)],
+        scratch_shapes=[v((3,d,d),low),v((d,d),low),v((FEED_GROUPS,d,group),low),v((FEED_GROUPS,group,d),low),
+            v((t,d),low),v((t,3*d),low),v((t,d),low),v((t,d),f32),v((t,d),f32),v((t,d),low),
+            v((FEED_GROUPS,t,group),f32),v((FEED_GROUPS,t,group),low),v((t,d),f32),v((t,d),f32),v((t,d),low),
+            pltpu.SemaphoreType.DMA((4+2*FEED_GROUPS,)),pltpu.SemaphoreType.DMA((9+2*FEED_GROUPS,))],
+        compiler_params=pltpu.CompilerParams(vmem_limit_bytes=LAYER_VMEM),
+        cost_estimate=pl.CostEstimate(flops=2*t*d*(4*d+2*ff)+4*t*t*d,bytes_accessed=2*d*(4*d+2*ff)+t*(30*d+6*ff),transcendentals=t*(ff+HEADS*t)),
+        )(x,mod,*weights)
+def backward_layer(g,mod,x,kept,weights):
+    _,project,_,branch,middle,_,u,_,feed_out=kept
+    _,_,w1,_=weights
+    t,d=x.shape; ff=w1.shape[1]; group=ff//FEED_GROUPS
+    made=lambda width,dtype: jax.ShapeDtypeStruct((t,width),dtype)
+    f32=jnp.float32
+    v=pltpu.VMEM
+    any_=pl.BlockSpec(memory_space=pl.ANY); inside=pl.BlockSpec(memory_space=pltpu.VMEM)
+    return pl.pallas_call(backward_kernel,in_specs=[inside]*3+[any_]*9,out_specs=[inside]+[any_]*6,
+        out_shape=[jax.ShapeDtypeStruct((1,6*d),f32),made(d,low),made(ff,low),made(d,low),made(3*d,low),made(d,f32),made(d,low)],
+        scratch_shapes=[v((t,d),f32),v((t,d),f32),v((t,d),f32),v((FEED_GROUPS,t,group),f32),v((t,3*d),low),
+            v((d,3*d),low),v((d,d),low),v((FEED_GROUPS,d,group),low),v((FEED_GROUPS,group,d),low),
+            v((t,d),low),v((FEED_GROUPS,t,group),low),v((t,d),low),v((t,d),low),v((t,3*d),low),v((t,d),f32),v((t,d),f32),v((t,d),low),
+            pltpu.SemaphoreType.DMA((6+3*FEED_GROUPS,)),pltpu.SemaphoreType.DMA((5+FEED_GROUPS,))],
+        compiler_params=pltpu.CompilerParams(vmem_limit_bytes=LAYER_VMEM),
+        cost_estimate=pl.CostEstimate(flops=2*t*d*(4*d+2*ff)+10*t*t*d,bytes_accessed=2*d*(4*d+2*ff)+t*(30*d+6*ff),transcendentals=t*(ff+HEADS*t)),
+        )(g,mod,x,feed_out,middle,branch,u,project,*weights)
 
 
 def matmul(left, right):
@@ -156,103 +238,6 @@
     return lax.dot_general(
         left, right, (((1,), (1,)), ((), ())), preferred_element_type=jnp.float32
     )
-
-
-def forward_layer(input_rows, modulation, weights):
-    query_key_value_weight, attention_output_weight, feed_first_weight, feed_second_weight = weights
-    batch_size, length, model_width = input_rows.shape
-    tokens = batch_size * length
-    shift_one, scale_one, gate_one, shift_two, scale_two, gate_two = modulation
-    normed_one, _ = center_scale(input_rows)
-    first_in = (normed_one * (1.0 + scale_one) + shift_one).astype(low).reshape(tokens, model_width)
-    project = matmul(first_in, query_key_value_weight).astype(low)
-    attended = attention(project, length)
-    branch = matmul(attended, attention_output_weight).reshape(batch_size, length, model_width)
-    middle_state = input_rows + gate_one * branch
-    normed_two, _ = center_scale(middle_state)
-    second_in = (
-        (normed_two * (1.0 + scale_two) + shift_two).astype(low).reshape(tokens, model_width)
-    )
-    shape = (batch_size, length, model_width)
-    hidden_pre, hidden, feed_out, result, result_low = mlp(
-        second_in,
-        middle_state.reshape(tokens, model_width),
-        gate_two.reshape(1, model_width),
-        feed_first_weight,
-        feed_second_weight,
-    )
-    feed_out, result, result_low = (
-        value.reshape(shape) for value in (feed_out, result, result_low)
-    )
-    kept = (
-        first_in,
-        project,
-        attended,
-        branch,
-        middle_state,
-        second_in,
-        hidden_pre,
-        hidden,
-        feed_out,
-    )
-    return result, result_low, kept
-
-
-def backward_layer(input_rows, modulation, weights, kept, grad_result):
-    query_key_value_weight, attention_output_weight, feed_first_weight, feed_second_weight = weights
-    (
-        first_in,
-        project,
-        attended,
-        branch,
-        middle_state,
-        second_in,
-        hidden_pre,
-        hidden,
-        feed_out,
-    ) = kept
-    batch_size, length, model_width = input_rows.shape
-    tokens = batch_size * length
-    _, scale_one, gate_one, _, scale_two, gate_two = modulation
-    grad_gate_two = jnp.sum(grad_result * feed_out, axis=1)
-    grad_feed = (gate_two * grad_result).astype(low).reshape(tokens, model_width)
-    grad_pre, grad_second = mlp_back(
-        grad_feed, feed_first_weight, feed_second_weight, hidden_pre
-    )
-    grad_second = grad_second.reshape(batch_size, length, model_width)
-    normed_two, inv_two = center_scale(middle_state)
-    grad_shift_two = jnp.sum(grad_second, axis=1)
-    grad_scale_two = jnp.sum(grad_second * normed_two, axis=1)
-    grad_middle = grad_result + norm_back(normed_two, inv_two, grad_second * (1.0 + scale_two))
-    grad_gate_one = jnp.sum(grad_middle * branch, axis=1)
-    grad_branch = (gate_one * grad_middle).astype(low).reshape(tokens, model_width)
-    grad_att = matmul_t(grad_branch, attention_output_weight).astype(low)
-    grad_project = attention_back(project, grad_att, length)
-    grad_first = matmul_t(grad_project, query_key_value_weight).reshape(
-        batch_size, length, model_width
-    )
-    normed_one, inv_one = center_scale(input_rows)
-    grad_shift_one = jnp.sum(grad_first, axis=1)
-    grad_scale_one = jnp.sum(grad_first * normed_one, axis=1)
-    grad_inputs = grad_middle + norm_back(normed_one, inv_one, grad_first * (1.0 + scale_one))
-    grad_mod = jnp.concatenate(
-        [
-            grad_shift_one,
-            grad_scale_one,
-            grad_gate_one,
-            grad_shift_two,
-            grad_scale_two,
-            grad_gate_two,
-        ],
-        axis=-1,
-    ).astype(low)
-    pairs = (
-        (hidden, grad_feed),
-        (second_in, grad_pre),
-        (attended, grad_branch),
-        (first_in, grad_project),
-    )
-    return grad_inputs, grad_mod, pairs
 
 
 def bits_of(count):
@@ -316,9 +301,16 @@
 
 MESH=pl.DeviceIdType.MESH
 
-def gather_kernel(shards,reps,count,*refs):
-    ins=refs[:count]; outs=refs[count:2*count]; bounce=refs[2*count:3*count]
-    line_send,line_recv,rep_send,rep_recv,local_in,local_out=refs[3*count:]
+def gather_kernel(shards,reps,arrays,chunks,*refs):
+    ins=refs[:arrays]; outs=refs[arrays:2*arrays]; bounce=refs[2*arrays:3*arrays]
+    line_send,line_recv,rep_send,rep_recv,local_in,local_out=refs[3*arrays:]
+    count=len(chunks)
+    def own_piece(c,rep):
+        index,rows,columns=chunks[c]
+        return ins[index].at[rep,rows,columns]
+    def piece_of(c,owner,rep):
+        index,rows,columns=chunks[c]
+        return outs[index].at[owner,rep,rows,columns]
     s=lax.axis_index("shard"); r=lax.axis_index("rep")
     bits=reps.bit_length()-1
     barrier=pltpu.get_barrier_semaphore()
@@ -329,32 +321,32 @@
             pl.semaphore_signal(barrier,inc=1,device_id={"shard":s+side},device_id_type=MESH)
     for bit in range(bits):
         pl.semaphore_signal(barrier,inc=1,device_id={"rep":r^(1<<bit)},device_id_type=MESH)
-    for c in range(count):
+    for c in range(arrays):
         pltpu.make_async_copy(ins[c],bounce[c],local_in.at[c]).start()
     pl.semaphore_wait(barrier,bits+jnp.minimum(s,1)+jnp.minimum(shards-1-s,1))
     sides=((0,1),(1,-1))
 
     def line(way,step,hop,c,owner):
-        src=ins[c].at[r] if hop==0 else outs[c].at[owner,r]
-        return pltpu.make_async_remote_copy(src_ref=src,dst_ref=outs[c].at[owner,r],
+        src=own_piece(c,r) if hop==0 else piece_of(c,owner,r)
+        return pltpu.make_async_remote_copy(src_ref=src,dst_ref=piece_of(c,owner,r),
             send_sem=line_send.at[way,hop,c],recv_sem=line_recv.at[way,hop,c],
             device_id={"shard":s+step},device_id_type=MESH)
     def side_copy(bit,mask,c,owner):
-        piece=outs[c].at[owner,r^mask]
+        piece=piece_of(c,owner,r^mask)
         return pltpu.make_async_remote_copy(src_ref=piece,dst_ref=piece,
             send_sem=rep_send.at[bit,mask,owner,c],recv_sem=rep_recv.at[mask|(1<<bit),owner,c],
             device_id={"rep":r^(1<<bit)},device_id_type=MESH)
     def low_bit(mask): return bits if mask==0 else (mask&-mask).bit_length()-1
     def arrived(mask,c,owner):
         bit=low_bit(mask)
-        piece=outs[c].at[owner,r^mask]
+        piece=piece_of(c,owner,r^mask)
         pltpu.make_async_remote_copy(src_ref=piece,dst_ref=piece,send_sem=rep_send.at[bit,mask^(1<<bit),owner,c],
             recv_sem=rep_recv.at[mask,owner,c],device_id={"rep":r^(1<<bit)},device_id_type=MESH).wait_recv()
     for c in range(count):
         for way,step in sides:
             @pl.when((s+step>=0)&(s+step<shards))
             def _(): line(way,step,0,c,s).start()
-    for c in range(count):
+    for c in range(arrays):
         pltpu.make_async_copy(ins[c],bounce[c],local_in.at[c]).wait()
         pltpu.make_async_copy(bounce[c],outs[c].at[s],local_out.at[c]).start()
     events=[(hop,c) for hop in range(1,shards) for c in range(count)]
@@ -400,21 +392,29 @@
         for way,step in sides:
             @pl.when((s+step>=0)&(s+step<shards))
             def _(): line(way,step,0,c,s).wait_send()
+    for c in range(arrays):
         pltpu.make_async_copy(bounce[c],outs[c].at[s],local_out.at[c]).wait()
 
 def gather_all(weights):
     shards=lax.axis_size("shard"); reps=lax.axis_size("rep"); bits=reps.bit_length()-1
     assert 1<<bits==reps
-    count=len(weights)
+    arrays=len(weights)
     views=[w.reshape(reps,w.shape[0]//reps,w.shape[1]) for w in weights]
+    def split(index,columns=None,rows=None):
+        depth,width=views[index].shape[1:]
+        return (index,slice(*(rows or (0,depth))),slice(*(columns or (0,width))))
+    deep=views[3].shape[1]; halves=((0,deep//2),(deep//2,deep)) if deep%16==0 else ((0,deep),)
+    chunks=[split(1),split(0,(D,3*D)),split(2,(0,2*D)),split(2,(2*D,4*D))]
+    chunks+=[split(3,rows=half) for half in halves]+[split(0,(0,D))]
+    count=len(chunks)
     any_=pl.BlockSpec(memory_space=pl.ANY)
-    outs=pl.pallas_call(functools.partial(gather_kernel,shards,reps,count),
-        in_specs=[any_]*count,out_specs=[any_]*count,
+    outs=pl.pallas_call(functools.partial(gather_kernel,shards,reps,arrays,chunks),
+        in_specs=[any_]*arrays,out_specs=[any_]*arrays,
         out_shape=[jax.ShapeDtypeStruct((shards,)+v.shape,v.dtype) for v in views],
         scratch_shapes=[pltpu.VMEM(v.shape,v.dtype) for v in views]+[
             pltpu.SemaphoreType.DMA((2,shards-1,count)),pltpu.SemaphoreType.DMA((2,shards-1,count)),
             pltpu.SemaphoreType.DMA((bits,reps,shards,count)),pltpu.SemaphoreType.DMA((reps,shards,count)),
-            pltpu.SemaphoreType.DMA((count,)),pltpu.SemaphoreType.DMA((count,))],
+            pltpu.SemaphoreType.DMA((arrays,)),pltpu.SemaphoreType.DMA((arrays,))],
         compiler_params=pltpu.CompilerParams(collective_id=1,has_side_effects=True),
         )(*views)
     return tuple(o.reshape(shards*w.shape[0],w.shape[1]) for o,w in zip(outs,weights))
@@ -435,16 +435,21 @@
     return pairs
 
 def reduce_kernel(blocks,*refs):
-    ins=(refs[:8],refs[8:16]); note,ada,outs,notes,act_out=refs[16],refs[17],refs[18:22],refs[22],refs[23]
+    ins=(refs[:8],refs[8:16]); parts,ada,outs,notes,act_out=refs[16:19],refs[19],refs[20:24],refs[24],refs[25]
     (left,right,left_sem,right_sem,part,came,send_sem,recv_sem,kept,final,
      final_sem,near_send,near_recv,far_send,far_recv,fwd_send,fwd_recv,note_send,note_recv,
-     notes_in,ada_in,ada_sem,_,blocks_out,blocks_in,act_send,act_recv)=unpack(refs[24:])
+     notes_in,ada_in,ada_sem,_,blocks_out,blocks_in,act_send,act_recv,note)=unpack(refs[26:])
     c=lax.axis_index("section")
     s=lax.axis_index("shard"); r=lax.axis_index("rep")
     bit={"s1":s//2,"s0":lax.rem(s,2),"r1":r//2,"r0":lax.rem(r,2)}
     peer={"s1":{"shard":lax.rem(s+2,4)},"s0":{"shard":s+1-2*lax.rem(s,2)},
           "r1":{"rep":lax.rem(r+2,4)},"r0":{"rep":r+1-2*lax.rem(r,2)}}
     across=lax.rem(r+2,4)
+    one,two,act=(part[...] for part in parts)
+    ours=jnp.concatenate([jnp.where(c==0,one,two),jnp.where(c==0,two,one)],axis=0).astype(low)
+    note[:,:6*D]=ours
+    note[:,6*D:]=act
+    notes_in[s*4+r]=jnp.concatenate([ours,act],axis=1)
     barrier=pltpu.get_barrier_semaphore()
     others=[(a,b) for a in range(4) for b in range(4) if a or b]
     def note_copy(index,a,b):
@@ -469,7 +474,6 @@
     pltpu.make_async_copy(ada,ada_in,ada_sem).start()
     pl.semaphore_wait(barrier,len(others)+4)
     for index,(a,b) in enumerate(others): note_copy(index,a,b).start()
-    notes_in[s*4+r]=note[...]
     def act_copy(index,a,other):
         section=1-c if other else c
         return pltpu.make_async_remote_copy(src_ref=blocks_out.at[s^a],dst_ref=blocks_in.at[c,s],send_sem=act_send.at[index],
@@ -601,7 +605,7 @@
     kept=[(refs[0],refs[0]),(refs[1],refs[2]),(refs[3],refs[4])]; refs=refs[5:]
     return (left,right,left_sem,right_sem,part,came,send,recv,kept,*refs)
 
-def reduce_all(halves,note,ada):
+def reduce_all(halves,grad_mods,act,ada):
     shards=lax.axis_size("shard"); reps=lax.axis_size("rep")
     rows=D//(shards*reps); group=D//shards
     blocks=12; units=3*blocks
@@ -620,12 +624,12 @@
     dma=pltpu.SemaphoreType.DMA
     keep=[lag+1 for lag in LAGS]
     inside=pl.BlockSpec(memory_space=pltpu.VMEM)
-    batch=note.shape[0]
+    batch=act.shape[0]; wide=7*D
     made=lambda shape,dtype: jax.ShapeDtypeStruct(shape,dtype)
     *grads,notes,act_grad=pl.pallas_call(functools.partial(reduce_kernel,blocks),
-        in_specs=[any_]*16+[inside,any_],out_specs=[any_]*4+[inside,inside],
+        in_specs=[any_]*16+[inside]*3+[any_],out_specs=[any_]*4+[inside,inside],
         out_shape=[made((reps,rows,3*D),low),made((reps,rows,D),low),made((reps,rows,4*D),low),made((4,reps,rows,D),low),
-            made((shards*reps*batch,note.shape[1]),low),made((shards,batch,group),jnp.float32)],
+            made((shards*reps*batch,wide),low),made((shards,batch,group),jnp.float32)],
         scratch_shapes=[
             pltpu.VMEM((2,shards,group,tokens),low),pltpu.VMEM((2,tokens,D),low),dma((2,)),dma((2,)),
             vm(keep[0],two(4)),
@@ -634,11 +638,11 @@
             vm(keep[1],two(3)),vm(keep[2],two(2)),vm(keep[2],two(2)),vm(keep[3],two(1)),vm(keep[3],two(1)),
             vm(5,piece),
             *[dma((units,)) for _ in range(7)],dma((15,)),dma((15,)),
-            pltpu.VMEM((shards*reps,)+note.shape,low),pltpu.VMEM(ada.shape,low),dma(()),dma(()),
-            pltpu.VMEM((shards,batch,group),jnp.float32),pltpu.VMEM((2,shards,batch,group),jnp.float32),dma((7,)),dma((7,))],
+            pltpu.VMEM((shards*reps,batch,wide),low),pltpu.VMEM(ada.shape,low),dma(()),dma(()),
+            pltpu.VMEM((shards,batch,group),jnp.float32),pltpu.VMEM((2,shards,batch,group),jnp.float32),dma((7,)),dma((7,)),pltpu.VMEM((batch,wide),low)],
         compiler_params=pltpu.CompilerParams(collective_id=2,has_side_effects=True),
         cost_estimate=pl.CostEstimate(flops=2*tokens*D*D*blocks,bytes_accessed=4*tokens*D*blocks,transcendentals=0),
-        )(*operands,note,ada)
+        )(*operands,*grad_mods,act,ada)
     grads=[grad.reshape(-1,grad.shape[-1]).astype(jnp.float32) for grad in grads]
     return grads,notes,act_grad
 
@@ -672,14 +676,6 @@
         total = total + lax.ppermute(
             partial[step], "shard", [(i, (i - step) % shards) for i in range(shards)]
         )
-    def pick(section_zero, section_one):
-        rows_of = jnp.where(
-            first_section,
-            total[section_zero : section_zero + 1],
-            total[section_one : section_one + 1],
-        )
-        return jnp.split(rows_of[:, None, :], 6, axis=-1)
-
     weights = gather_all(
         (
             query_key_value_weight[0],
@@ -691,40 +687,44 @@
 
     forth = [(0, 1)]
     back = [(1, 0)]
-    latent = (latents[:1], latents[1:])
-    grad_out = (cotangent[:1], cotangent[1:])
-    mod_zero, mod_one, mod_two = pick(0, 0), pick(1, 0), pick(0, 1)
-    _, early, _ = forward_layer(latent[0].astype(jnp.float32), mod_zero, weights)
-    incoming = lax.ppermute(early, "section", forth)
-    input_one = jnp.where(first_section, latent[1], incoming).astype(jnp.float32)
-    result_one, sent, kept_one = forward_layer(input_one, mod_one, weights)
+    swapped = jnp.where(first_section, total[1:], total[:1])
+    straight = jnp.where(first_section, total[:1], total[1:])
+    *_, sent = forward_layer(latents[0], total[:1], weights)
     incoming = lax.ppermute(sent, "section", forth)
-    early, _, _ = backward_layer(
-        input_one, mod_one, weights, kept_one, grad_out[0].astype(jnp.float32)
+    input_one = jnp.where(first_section, latents[1], incoming)
+    *kept_one, result_one, sent = forward_layer(input_one, swapped, weights)
+    incoming = lax.ppermute(sent, "section", forth)
+    *_, sent = backward_layer(cotangent[0], swapped, input_one, kept_one, weights)
+    returning = lax.ppermute(sent, "section", back)
+    incoming, sent = lax.optimization_barrier((incoming, sent))
+    input_two = jnp.where(first_section, latents[0], incoming)
+    *kept_two, result_two, _ = forward_layer(input_two, straight, weights)
+    grad_result = jnp.where(first_section, returning, cotangent[1])
+    mod_one, *grads_one, grad_in_one, sent = backward_layer(
+        grad_result, straight, input_two, kept_two, weights
     )
-    early = early.astype(low)
-    returning = lax.ppermute(early, "section", back)
-    incoming, early = lax.optimization_barrier((incoming, early))
-    input_two = jnp.where(first_section, latent[0], incoming).astype(jnp.float32)
-    result_two, _, kept_two = forward_layer(input_two, mod_two, weights)
-    grad_result = jnp.where(first_section, returning, grad_out[1]).astype(jnp.float32)
-    grad_in_one, grad_mod_one, pairs_one = backward_layer(
-        input_two, mod_two, weights, kept_two, grad_result
+    returning = lax.ppermute(sent, "section", back)
+    grad_result = jnp.where(first_section, returning, cotangent[0])
+    mod_two, *grads_two, grad_in_two, _ = backward_layer(
+        grad_result, swapped, input_one, kept_one, weights
     )
-    returning = lax.ppermute(grad_in_one.astype(low), "section", back)
-    grad_result = jnp.where(first_section, returning, grad_out[0]).astype(jnp.float32)
-    grad_in_two, grad_mod_two, pairs_two = backward_layer(
-        input_one, mod_one, weights, kept_one, grad_result
-    )
-    grad_mod = jnp.where(
-        first_section,
-        jnp.concatenate([grad_mod_one, grad_mod_two], axis=0),
-        jnp.concatenate([grad_mod_two, grad_mod_one], axis=0),
-    )
-    packed = jnp.concatenate([grad_mod, act], axis=-1)
+
+    def products(kept, grads):
+        first_in, _, attended, _, _, second_in, _, hidden, _ = kept
+        grad_feed, grad_pre, grad_branch, grad_project = grads
+        return (
+            (hidden, grad_feed),
+            (second_in, grad_pre),
+            (attended, grad_branch),
+            (first_in, grad_project),
+        )
+
+    kept_one, kept_two, _ = lax.optimization_barrier((kept_one, kept_two, sent))
+    pairs_one, pairs_two = products(kept_two, grads_one), products(kept_one, grads_two)
+    wide = mod_one.shape[1]
     if shards == 4 and reps == 4:
         (grad_qkv, grad_wout, grad_fc1, grad_fc2), packed, act_grad = reduce_all(
-            (pairs_one, pairs_two), packed, modulation_weight
+            (pairs_one, pairs_two), (mod_one, mod_two), act, modulation_weight
         )
         act_total = act_grad.transpose(1, 0, 2).reshape(batch, shards * rows)
     else:
@@ -736,9 +736,15 @@
         grad_fc1 = reduce_rows(*pairs[1], False)
         grad_wout = reduce_rows(*pairs[2], True)
         grad_qkv = reduce_rows(*pairs[3], True)
+        grad_mod = jnp.where(
+            first_section,
+            jnp.concatenate([mod_one, mod_two], axis=0),
+            jnp.concatenate([mod_two, mod_one], axis=0),
+        ).astype(low)
+        packed = jnp.concatenate([grad_mod, act], axis=-1)
         packed = lax.all_gather(packed, ("shard", "rep"), axis=0, tiled=True)
         own_mod = lax.dynamic_index_in_dim(
-            packed[:, : grad_mod.shape[1]].reshape(shards, reps, batch, -1), rep, 1, keepdims=False
+            packed[:, : wide].reshape(shards, reps, batch, -1), rep, 1, keepdims=False
         ).reshape(shards * batch, -1)
         act_grad = matmul_t(own_mod, modulation_weight)
         act_grad = act_grad + lax.ppermute(act_grad, "section", [(0, 1), (1, 0)])
@@ -750,16 +756,15 @@
             )
         act_total = act_total.transpose(1, 0, 2).reshape(batch, shards * rows)
 
-    boundary = jnp.concatenate(
+    boundary = jnp.stack(
         [
             jnp.where(first_section, grad_in_one, result_one),
             jnp.where(first_section, grad_in_two, result_two),
-        ],
-        axis=0,
+        ]
     )[None]
 
-    all_mod = packed[:, : grad_mod.shape[1]]
-    all_act = packed[:, grad_mod.shape[1] :]
+    all_mod = packed[:, : wide]
+    all_act = packed[:, wide :]
     act_rows = lax.dynamic_slice_in_dim(all_act, shard * rows, rows, 1)
     grad_ada = lax.dot_general(
         act_rows, all_mod, (((0,), (0,)), ((), ())), preferred_element_type=jnp.float32

time: 698 us -> 574 us (0.82); the launches traced: 688 us -> 571 us
  matrix products: 66.3 us -> 7.43 us
  other arithmetic: 59.2 us -> 20 us
  local copies, waits for them, and re-layouts: 27.9 us -> 17.8 us
    dot_general x7 -> x1, matrix products: 33.2 us -> 2.88 us  [matmul(): return jnp.dot(left, right, preferred_element_type=jnp.float32)]
    dot_general x6 -> x0, matrix products: 28.6 us -> none  [matmul_t(): lax.dot_general(left, right, (((1,), (1,)), ((), ())), preferred_element_...]
    reduce_sum x21 -> x0, other arithmetic: 24.2 us -> none  [the longest x2 4.63 us: backward_layer(): grad_scale_two = jnp.sum(grad_second * normed_two, axis=1)]
    ppermute x3 -> x2, waiting for transfers between devices: 19.1 us -> 0.67 us  [body(): returning = lax.ppermute(sent, 'section', back)]
    ppermute x1 -> x2, waiting for transfers between devices: 0.01 us -> 12.5 us  [body(): incoming = lax.ppermute(sent, 'section', forth)]
    unnamed x186 -> x38, local copies, waits for them, and re-layouts: 10.1 us -> 0.91 us
    reshape x9 -> x0, other arithmetic: 8.58 us -> none  [the longest x3 3.93 us: backward_layer(): (gate_two * grad_result).astype(low).reshape(tokens, model_width)]
    pallas_call x13 -> x7, Pallas kernels: 290 us -> 288 us  [the longest x1 148 us: gather_all(): pl.pallas_call(functools.partial(gather_kernel, shards, reps, arrays, chu...]
  transfers between devices with their start and end apart: 10 -> 10, of which waited for: 4 -> 4; matrix products, arithmetic and copies ran while one was open for 7% -> 3% of each run, Pallas kernels for 27% -> 34%
where the time goes in v1:
time: 574 us; the launch traced here: 571 us
  Pallas kernels  486 us (85%)
  starting transfers between devices  20.6 us (4%)
  other arithmetic  20 us (3%)
  local copies, waits for them, and re-layouts  17.8 us (3%)
  waiting for transfers between devices  17.5 us (3%)
  matrix products  7.43 us (1%)
    pallas_call x1, Pallas kernels, reduce_all(): pl.pallas_call(functools.partial(reduce_kernel, blocks), in_specs=[any_]...  198 us
    pallas_call x1, Pallas kernels, gather_all(): pl.pallas_call(functools.partial(gather_kernel, shards, reps, arrays, chu...  148 us
    pallas_call x3, Pallas kernels, backward_layer(): pl.pallas_call(backward_kernel, in_specs=[inside] * 3 + [any_] * 9, out_s...  83.1 us
    pallas_call x3, Pallas kernels, forward_layer(): pl.pallas_call(forward_kernel, in_specs=[inside, inside] + [any_] * 4, ou...  56.4 us
    ppermute x2, waiting for transfers between devices, body(): incoming = lax.ppermute(sent, 'section', forth)  12.5 us
  transfers between devices with their start and end apart: 10, of which 4 were waited for; matrix products, arithmetic and copies ran while one was open for 3% of the time, Pallas kernels for 34%

profile of v1, /device:TPU:0, one launch (start us, length us, event | category | flops | bytes accessed | tf_op | source)
XLA Modules:
  0.0 570.9 jit_solution(2695050086160387145)
XLA Ops:
  0.7 0.7 fusion.7.refs_18_
  1.5 5.1 collective-permute-start.2
  6.7 1.0 collective-permute-start.1
  7.7 0.3 collective-permute-done.2
  8.0 4.1 collective-permute-done
  12.1 2.9 fusion.10
  15.0 3.0 collective-permute-start.3
  18.0 0.6 collective-permute-start.4
  18.6 0.9 slice_bitcast_fusion.x_ref
  19.5 148.4 %shard_map.135 = (bf16[4,4,72,3456]{3,2,1,0:T(8,128)(2,1)}, bf16[4,4,72,1152]{3,2,1,0:T(8,128)(2,1)}, bf16[4,4,72,4608]{3,2,1,0:T(8,128)(2,1)}, bf16[4,4,288,1152]{3,2,1,0:T(8,128)(2,1)}) custom-call(bf16[4,72,3456]{2,1,0:T(8,128)(2,1)} %bitcast.108, bf16[4,72,1152]{2,1,0:T(8,128)(2,1)} %bitcast.110, bf16[4,72,4608]{2,1,0:T(8,128)(2,1)} %bitcast.99, ...), custom_call_target="tpu_custom_call" | custom-call | tf_op jit(solution)/shard_map/pallas_call | solution.py:411
  168.0 0.7 broadcast_select_fusion.2
  168.7 19.0 %shard_map.136 = (bf16[256,1152]{1,0:T(8,128)(2,1)}, bf16[256,3456]{1,0:T(8,128)(2,1)}, bf16[256,1152]{1,0:T(8,128)(2,1)}, f32[256,1152]{1,0:T(8,128)}, f32[256,...) custom-call(bf16[256,1152]{1,0:T(8,128)(2,1)} %slice_bitcast_fusion., ...), custom_call_target="tpu_custom_call" | custom-call | flops 8455716864 | bytes 47775744 | tf_op jit(solution)/shard_map/pallas_call | solution.py:205
  187.7 3.4 collective-permute-start.6
  191.1 0.9 slice_bitcast_fusion.1.g_ref
  192.0 12.5 %collective-permute-done.6 = bf16[256,1152]{1,0:T(8,128)(2,1)S(1)} collective-permute-done((bf16[256,1152]{1,0:T(8,128)(2,1)}, bf16[256,1152]{1,0:T(8,128)(2,1)S(1)}, u32[]{:S(2)}, u32[]{:S(2)}) %collective-permute-start.6) | collective-permute-done | bytes 589856 | tf_op jit(solution)/shard_map/ppermute | solution.py:693
  204.5 0.9 bitcast_select_fusion.1.x_ref
  205.4 18.7 %shard_map.137 = (bf16[256,1152]{1,0:T(8,128)(2,1)}, bf16[256,3456]{1,0:T(8,128)(2,1)}, bf16[256,1152]{1,0:T(8,128)(2,1)}, f32[256,1152]{1,0:T(8,128)}, f32[256,...) custom-call(bf16[256,1152]{1,0:T(8,128)(2,1)} %bitcast_select_fusion, ...), custom_call_target="tpu_custom_call" | custom-call | flops 8455716864 | bytes 47775744 | tf_op jit(solution)/shard_map/pallas_call | solution.py:205
  224.2 4.7 collective-permute-start.8
  228.9 27.6 %shard_map.138 = (f32[1,6912]{1,0:T(1,128)}, bf16[256,1152]{1,0:T(8,128)(2,1)}, bf16[256,4608]{1,0:T(8,128)(2,1)}, bf16[256,1152]{1,0:T(8,128)(2,1)}, bf16[256,3...) custom-call(bf16[256,1152]{1,0:T(8,128)(2,1)} %slice_bitcast_fusion.1.g_ref, ...), custom_call_target="tpu_custom_call" | custom-call | flops 8908701696 | bytes 47775744 | tf_op jit(solution)/shard_map/pallas_call | solution.py:222
  256.5 1.3 collective-permute-start.7
  257.8 0.9 broadcast_select_fusion.1.x_ref
  258.7 18.7 %shard_map.139 = (bf16[256,1152]{1,0:T(8,128)(2,1)}, bf16[256,3456]{1,0:T(8,128)(2,1)}, bf16[256,1152]{1,0:T(8,128)(2,1)}, f32[256,1152]{1,0:T(8,128)}, f32[256,...) custom-call(bf16[256,1152]{1,0:T(8,128)(2,1)} %broadcast_select_fusi, ...), custom_call_target="tpu_custom_call" | custom-call | flops 8455716864 | bytes 47775744 | tf_op jit(solution)/shard_map/pallas_call | solution.py:205
  277.4 0.9 bitcast_select_fusion.g_ref
  278.3 27.7 %shard_map.140 = (f32[1,6912]{1,0:T(1,128)}, bf16[256,1152]{1,0:T(8,128)(2,1)}, bf16[256,4608]{1,0:T(8,128)(2,1)}, bf16[256,1152]{1,0:T(8,128)(2,1)}, bf16[256,3...) custom-call(bf16[256,1152]{1,0:T(8,128)(2,1)} %bitcast_select_fusion.g_ref, ...), custom_call_target="tpu_custom_call" | custom-call | flops 8908701696 | bytes 47775744 | tf_op jit(solution)/shard_map/pallas_call | solution.py:222
  306.1 1.4 collective-permute-start.9
  307.5 1.1 copy.28
  308.6 1.1 copy.29
  309.7 1.1 copy.30
  310.8 1.1 copy.32
  311.9 1.1 copy.33
  312.9 1.1 copy.34
  314.0 4.4 copy.31
  318.4 2.4 copy.35
  320.8 1.4 select_bitcast_fusion.1
  322.2 0.7 collective-permute-done.9
  322.9 2.0 broadcast_select_fusion.g_ref
  324.9 27.8 %shard_map.141 = (f32[1,6912]{1,0:T(1,128)}, bf16[256,1152]{1,0:T(8,128)(2,1)}, bf16[256,4608]{1,0:T(8,128)(2,1)}, bf16[256,1152]{1,0:T(8,128)(2,1)}, bf16[256,3...) custom-call(bf16[256,1152]{1,0:T(8,128)(2,1)} %broadcast_select_fusion.g_ref, ...), custom_call_target="tpu_custom_call" | custom-call | flops 8908701696 | bytes 47775744 | tf_op jit(solution)/shard_map/pallas_call | solution.py:222
  352.6 198.4 %shard_map.142 = (bf16[4,72,3456]{2,1,0:T(8,128)(2,1)}, bf16[4,72,1152]{2,1,0:T(8,128)(2,1)}, bf16[4,72,4608]{2,1,0:T(8,128)(2,1)}, bf16[4,4,72,1152]{3,2,1,0:T(...) custom-call(bf16[4,288,256]{2,1,0:T(8,128)(2,1)} %bitcast.114, bf16[4,288,256]{2,1,0:T(8,128)(2,1)} %bitcast.115, ...), custom_call_target="tpu_custom_call" | custom-call | flops 16307453952 | bytes 28311552 | tf_op jit(solution)/shard_map/pallas_call | solution.py:629
  551.0 0.7 copy.36
  551.9 0.6 fusion.9
  552.5 0.9 slice.55
  553.4 2.2 bitcast_convert_fusion.2
  555.6 2.2 bitcast_convert_fusion.1
  557.8 0.8 copy-done.1
  558.7 3.0 bitcast_convert_fusion
  561.7 2.7 convert.7
  564.6 1.6 maximum_bitcast_fusion
  566.1 4.6 convolution_bitcast_fusion
  (51 shorter events, 0.6 us)
Async XLA Ops:
  1.4 13.5 %copy-start.16 = (bf16[2,1152]{1,0:T(2,128)(2,1)}, bf16[2,1152]{1,0:T(2,128)(2,1)S(1)}, u32[]{:S(2)}) copy-start(bf16[2,1152]{1,0:T(2,128)(2,1)S(1)} %fusion.7.refs_18_) | copy-start | bytes 13828
  1.5 6.4 %collective-permute-start.2 = (bf16[2,288]{1,0:T(2,128)(2,1)S(1)}, bf16[2,288]{1,0:T(2,128)(2,1)S(1)}, u32[]{:S(2)}, u32[]{:S(2)}) collective-permute-start(bf16[2,288]{1,0:T(2,128)(2,1)S(1)} %bitcast.125), channel_id=1, source_target_pairs={{0,12},{4,0},{8,4},{12,8},{1,13},{5,1},{9,5},{13,9},{2,14},{6,2},{... | collective-permute-start | bytes 3464 | tf_op jit(solution)/shard_map/ppermute | solution.py:297
  6.7 5.4 collective-permute-start
  6.7 5.4 collective-permute-start.1
  12.0 6.6 %copy-start.2 = (bf16[2,256,1152]{2,1,0:T(8,128)(2,1)S(1)}, bf16[2,256,1152]{2,1,0:T(8,128)(2,1)}, u32[]{:S(2)}) copy-start(bf16[2,256,1152]{2,1,0:T(8,128)(2,1)} %param.8) | copy-start | bytes 3538948
  15.0 153.0 %collective-permute-start.3 = (f32[2,6912]{1,0:T(2,128)S(1)}, f32[2,6912]{1,0:T(2,128)S(1)}, u32[]{:S(2)}, u32[]{:S(2)}) collective-permute-start(f32[2,6912]{1,0:T(2,128)S(1)} %get-tuple-element.117), channel_id=1, source_target_pairs={{0,12},{4,0},{8,4},{12,8},{1,13},{5,1},{9,5},{13,9},{2,14},{6,2},{... | collective-permute-start | bytes 165896 | tf_op jit(solution)/shard_map/ppermute | solution.py:676
  18.0 150.0 %collective-permute-start.5 = (f32[2,6912]{1,0:T(2,128)S(1)}, f32[2,6912]{1,0:T(2,128)S(1)}, u32[]{:S(2)}, u32[]{:S(2)}) collective-permute-start(f32[2,6912]{1,0:T(2,128)S(1)} %get-tuple-element.118), channel_id=1, source_target_pairs={{0,4},{4,8},{8,12},{12,0},{1,5},{5,9},{9,13},{13,1},{2,6},{6,10},{... | collective-permute-start | bytes 165896 | tf_op jit(solution)/shard_map/ppermute | solution.py:676
  18.0 150.0 %collective-permute-start.4 = (f32[2,6912]{1,0:T(2,128)S(1)}, f32[2,6912]{1,0:T(2,128)S(1)}, u32[]{:S(2)}, u32[]{:S(2)}) collective-permute-start(f32[2,6912]{1,0:T(2,128)S(1)} %get-tuple-element.119), channel_id=1, source_target_pairs={{0,8},{4,12},{8,0},{12,4},{1,9},{5,13},{9,1},{13,5},{2,10},{6,14},... | collective-permute-start | bytes 165896 | tf_op jit(solution)/shard_map/ppermute | solution.py:676
  168.7 22.4 %copy-start.3 = (bf16[2,256,1152]{2,1,0:T(8,128)(2,1)S(1)}, bf16[2,256,1152]{2,1,0:T(8,128)(2,1)}, u32[]{:S(2)}) copy-start(bf16[2,256,1152]{2,1,0:T(8,128)(2,1)} %param.15) | copy-start | bytes 3538948
  187.7 16.8 %collective-permute-start.6 = (bf16[256,1152]{1,0:T(8,128)(2,1)}, bf16[256,1152]{1,0:T(8,128)(2,1)S(1)}, u32[]{:S(2)}, u32[]{:S(2)}) collective-permute-start(bf16[256,1152]{1,0:T(8,128)(2,1)} %get-tuple-element.66), channel_id=1, source_target_pairs={{0,16},{1,17},{2,18},{3,19},{4,20},{5,21},{6,22},{7,23},{8,24},{9,... | collective-permute-start | bytes 1769480 | tf_op jit(solution)/shard_map/ppermute | solution.py:693
  224.2 33.7 %collective-permute-start.8 = (bf16[256,1152]{1,0:T(8,128)(2,1)}, bf16[256,1152]{1,0:T(8,128)(2,1)S(1)}, u32[]{:S(2)}, u32[]{:S(2)}) collective-permute-start(bf16[256,1152]{1,0:T(8,128)(2,1)} %get-tuple-element.73), channel_id=1, source_target_pairs={{0,16},{1,17},{2,18},{3,19},{4,20},{5,21},{6,22},{7,23},{8,24},{9,... | collective-permute-start | bytes 1769480 | tf_op jit(solution)/shard_map/ppermute | solution.py:696
  256.5 20.9 %collective-permute-start.7 = (bf16[256,1152]{1,0:T(8,128)(2,1)}, bf16[256,1152]{1,0:T(8,128)(2,1)S(1)}, u32[]{:S(2)}, u32[]{:S(2)}) collective-permute-start(bf16[256,1152]{1,0:T(8,128)(2,1)} %get-tuple-element.72), channel_id=1, source_target_pairs={{16,0},{17,1},{18,2},{19,3},{20,4},{21,5},{22,6},{23,7},{24,8},{25... | collective-permute-start | bytes 1769480 | tf_op jit(solution)/shard_map/ppermute | solution.py:698
  278.3 29.2 %copy-start.13 = (bf16[256,1152]{1,0:T(8,128)(2,1)S(1)}, bf16[256,1152]{1,0:T(8,128)(2,1)}, u32[]{:S(2)}) copy-start(bf16[256,1152]{1,0:T(8,128)(2,1)} %get-tuple-element.93) | copy-start | bytes 1769476
  278.3 30.3 %copy-start.12 = (bf16[256,1152]{1,0:T(8,128)(2,1)S(1)}, bf16[256,1152]{1,0:T(8,128)(2,1)}, u32[]{:S(2)}) copy-start(bf16[256,1152]{1,0:T(8,128)(2,1)} %get-tuple-element.94) | copy-start | bytes 1769476
  306.1 3.7 copy-start.11
  306.1 16.8 %collective-permute-start.9 = (bf16[256,1152]{1,0:T(8,128)(2,1)}, bf16[256,1152]{1,0:T(8,128)(2,1)}, u32[]{:S(2)}, u32[]{:S(2)}) collective-permute-start(bf16[256,1152]{1,0:T(8,128)(2,1)} %get-tuple-element.82), channel_id=1, source_target_pairs={{16,0},{17,1},{18,2},{19,3},{20,4},{21,5},{22,6},{23,7},{24,8},{25... | collective-permute-start | bytes 1769480 | tf_op jit(solution)/shard_map/ppermute | solution.py:706
  307.5 3.3 copy-start.10
  308.6 3.2 copy-start.9
  309.7 3.2 copy-start.8
  314.0 4.4 copy-start.4
  352.6 199.2 %copy-start.15 = (bf16[2,1152]{1,0:T(2,128)(2,1)S(1)}, bf16[2,1152]{1,0:T(2,128)(2,1)}, u32[]{:S(2)}) copy-start(bf16[2,1152]{1,0:T(2,128)(2,1)} %param.9) | copy-start | bytes 13828
  551.8 3.8 copy-start.5
  555.6 3.1 copy-start.1
  558.7 3.0 copy-start
  561.7 2.7 copy-start.6
  561.7 2.7 copy-start.7
  564.5 1.6 copy-start.14

commit v2 on v1

--- a/solution.py
+++ b/solution.py
@@ -302,8 +302,10 @@
 MESH=pl.DeviceIdType.MESH
 
 def gather_kernel(shards,reps,arrays,chunks,*refs):
-    ins=refs[:arrays]; outs=refs[arrays:2*arrays]; bounce=refs[2*arrays:3*arrays]
-    line_send,line_recv,rep_send,rep_recv,local_in,local_out=refs[3*arrays:]
+    ins=refs[:arrays]; act,ada=refs[arrays:arrays+2]; refs=refs[arrays+2:]
+    outs=refs[:arrays]; mod_out=refs[arrays]; refs=refs[arrays+1:]; bounce=refs[:arrays]
+    (line_send,line_recv,rep_send,rep_recv,local_in,local_out,
+     ada_v,acts_in,mod_send,mod_in,ada_sem,act_sems,mod_sems)=refs[arrays:]
     count=len(chunks)
     def own_piece(c,rep):
         index,rows,columns=chunks[c]
@@ -314,16 +316,22 @@
     s=lax.axis_index("shard"); r=lax.axis_index("rep")
     bits=reps.bit_length()-1
     barrier=pltpu.get_barrier_semaphore()
-    for side in (-1,1):
-        there=(s+side>=0)&(s+side<shards)
-        @pl.when(there)
-        def _():
-            pl.semaphore_signal(barrier,inc=1,device_id={"shard":s+side},device_id_type=MESH)
+    for other in range(1,shards):
+        pl.semaphore_signal(barrier,inc=1,device_id={"shard":s^other},device_id_type=MESH)
     for bit in range(bits):
         pl.semaphore_signal(barrier,inc=1,device_id={"rep":r^(1<<bit)},device_id_type=MESH)
     for c in range(arrays):
         pltpu.make_async_copy(ins[c],bounce[c],local_in.at[c]).start()
-    pl.semaphore_wait(barrier,bits+jnp.minimum(s,1)+jnp.minimum(shards-1-s,1))
+    pltpu.make_async_copy(ada,ada_v,ada_sem).start()
+    acts_in[s]=act[s]
+    pl.semaphore_wait(barrier,bits+shards-1)
+    def act_copy(other):
+        return pltpu.make_async_remote_copy(src_ref=act.at[s^other],dst_ref=acts_in.at[s],send_sem=act_sems.at[0,other-1],
+            recv_sem=act_sems.at[1,other-1],device_id={"shard":s^other},device_id_type=MESH)
+    def mod_copy(other):
+        return pltpu.make_async_remote_copy(src_ref=mod_send.at[s^other],dst_ref=mod_in.at[s],send_sem=mod_sems.at[0,other-1],
+            recv_sem=mod_sems.at[1,other-1],device_id={"shard":s^other},device_id_type=MESH)
+    for other in range(1,shards): act_copy(other).start()
     sides=((0,1),(1,-1))
 
     def line(way,step,hop,c,owner):
@@ -349,6 +357,14 @@
     for c in range(arrays):
         pltpu.make_async_copy(ins[c],bounce[c],local_in.at[c]).wait()
         pltpu.make_async_copy(bounce[c],outs[c].at[s],local_out.at[c]).start()
+    for other in range(1,shards): act_copy(other).wait()
+    pltpu.make_async_copy(ada,ada_v,ada_sem).wait()
+    acts=jnp.concatenate([acts_in[k].astype(jnp.float32) for k in range(shards)],axis=0).astype(low)
+    partial=dot(acts,ada_v[...])
+    batch=act.shape[1]
+    for k in range(shards): mod_send[k]=partial[k*batch:(k+1)*batch]
+    mod_in[s]=mod_send[s]
+    for other in range(1,shards): mod_copy(other).start()
     events=[(hop,c) for hop in range(1,shards) for c in range(count)]
     relays=[m for m in range(1,reps) if low_bit(m)>0]
     depth=max([m.bit_count() for m in relays],default=0)
@@ -394,8 +410,12 @@
             def _(): line(way,step,0,c,s).wait_send()
     for c in range(arrays):
         pltpu.make_async_copy(bounce[c],outs[c].at[s],local_out.at[c]).wait()
-
-def gather_all(weights):
+    for other in range(1,shards): mod_copy(other).wait()
+    total=mod_in[0]
+    for k in range(1,shards): total=total+mod_in[k]
+    mod_out[...]=total
+
+def gather_all(weights,act,ada):
     shards=lax.axis_size("shard"); reps=lax.axis_size("rep"); bits=reps.bit_length()-1
     assert 1<<bits==reps
     arrays=len(weights)
@@ -408,16 +428,21 @@
     chunks+=[split(3,rows=half) for half in halves]+[split(0,(0,D))]
     count=len(chunks)
     any_=pl.BlockSpec(memory_space=pl.ANY)
-    outs=pl.pallas_call(functools.partial(gather_kernel,shards,reps,arrays,chunks),
-        in_specs=[any_]*arrays,out_specs=[any_]*arrays,
-        out_shape=[jax.ShapeDtypeStruct((shards,)+v.shape,v.dtype) for v in views],
+    inside=pl.BlockSpec(memory_space=pltpu.VMEM)
+    batch=act.shape[1]
+    *outs,modulation=pl.pallas_call(functools.partial(gather_kernel,shards,reps,arrays,chunks),
+        in_specs=[any_]*arrays+[inside,any_],out_specs=[any_]*arrays+[inside],
+        out_shape=[jax.ShapeDtypeStruct((shards,)+v.shape,v.dtype) for v in views]+[jax.ShapeDtypeStruct((batch,ada.shape[1]),jnp.float32)],
         scratch_shapes=[pltpu.VMEM(v.shape,v.dtype) for v in views]+[
             pltpu.SemaphoreType.DMA((2,shards-1,count)),pltpu.SemaphoreType.DMA((2,shards-1,count)),
             pltpu.SemaphoreType.DMA((bits,reps,shards,count)),pltpu.SemaphoreType.DMA((reps,shards,count)),
-            pltpu.SemaphoreType.DMA((arrays,)),pltpu.SemaphoreType.DMA((arrays,))],
+            pltpu.SemaphoreType.DMA((arrays,)),pltpu.SemaphoreType.DMA((arrays,)),
+            pltpu.VMEM(ada.shape,low),pltpu.VMEM(act.shape,low),pltpu.VMEM((shards,batch,ada.shape[1]),jnp.float32),
+            pltpu.VMEM((shards,batch,ada.shape[1]),jnp.float32),pltpu.SemaphoreType.DMA(()),
+            pltpu.SemaphoreType.DMA((2,shards-1)),pltpu.SemaphoreType.DMA((2,shards-1))],
         compiler_params=pltpu.CompilerParams(collective_id=1,has_side_effects=True),
-        )(*views)
-    return tuple(o.reshape(shards*w.shape[0],w.shape[1]) for o,w in zip(outs,weights))
+        )(*views,act,ada)
+    return tuple(o.reshape(shards*w.shape[0],w.shape[1]) for o,w in zip(outs,weights)),modulation
 
 
 NAMES=("s1","s0","r1","r0")
@@ -668,21 +693,16 @@
 
     cond_float = cond.astype(jnp.float32)
     act = jax.nn.silu(cond_float).astype(low)
-    came = exchange_shards(act.reshape(batch, shards, rows).transpose(1, 0, 2))
-    partial = matmul(jnp.concatenate(came, axis=0), modulation_weight)
-    partial = partial.reshape(shards, batch, -1)
-    total = partial[0]
-    for step in range(1, shards):
-        total = total + lax.ppermute(
-            partial[step], "shard", [(i, (i - step) % shards) for i in range(shards)]
-        )
-    weights = gather_all(
+    blocks = act.reshape(batch, shards, rows).transpose(1, 0, 2)
+    weights, total = gather_all(
         (
             query_key_value_weight[0],
             attention_output_weight[0],
             feed_first_weight[0],
             feed_second_weight[0],
-        )
+        ),
+        blocks,
+        modulation_weight,
     )
 
     forth = [(0, 1)]

time: 574 us -> 572 us (level); the launches traced: 571 us -> 561 us
  starting transfers between devices: 20.6 us -> 10.9 us
    ppermute x6 -> x0, starting transfers between devices: 9.75 us -> none  [the longest x3 6.14 us: exchange_shards(): lax.ppermute(block, 'shard', [(i, (i + step) % count) for i in range(coun...]
    pallas_call x1, Pallas kernels: 148 us -> 155 us  [gather_all(): pl.pallas_call(functools.partial(gather_kernel, shards, reps, arrays, chu...]
  transfers between devices with their start and end apart: 10 -> 4, of which waited for: 4 -> 2; matrix products, arithmetic and copies ran while one was open for 3% -> 3% of each run, Pallas kernels for 34% -> 8%
where the time goes in v2:
time: 572 us; the launch traced here: 561 us
  Pallas kernels  491 us (86%)
  other arithmetic  20.8 us (4%)
  local copies, waits for them, and re-layouts  19.3 us (3%)
  waiting for transfers between devices  13.2 us (2%)
  starting transfers between devices  10.9 us (2%)
    pallas_call x1, Pallas kernels, reduce_all(): pl.pallas_call(functools.partial(reduce_kernel, blocks), in_specs=[any_]...  197 us
    pallas_call x1, Pallas kernels, gather_all(): pl.pallas_call(functools.partial(gather_kernel, shards, reps, arrays, chu...  155 us
    pallas_call x3, Pallas kernels, backward_layer(): pl.pallas_call(backward_kernel, in_specs=[inside] * 3 + [any_] * 9, out_s...  83.1 us
    pallas_call x3, Pallas kernels, forward_layer(): pl.pallas_call(forward_kernel, in_specs=[inside, inside] + [any_] * 4, ou...  56.4 us
    ppermute x2, waiting for transfers between devices, body(): incoming = lax.ppermute(sent, 'section', forth)  12.5 us
  transfers between devices with their start and end apart: 4, of which 2 were waited for; matrix products, arithmetic and copies ran while one was open for 3% of the time, Pallas kernels for 8%

profile of v2, /device:TPU:0, one launch (start us, length us, event | category | flops | bytes accessed | tf_op | source)
XLA Modules:
  0.0 561.1 jit_solution(849576835814282412)
XLA Ops:
  0.6 0.7 fusion.5.refs_18_
  1.4 0.1 reshape.108
  1.5 0.6 copy.26
  2.1 1.9 slice_bitcast_fusion.x_ref
  4.0 154.8 %shard_map.135 = (bf16[4,4,72,3456]{3,2,1,0:T(8,128)(2,1)}, bf16[4,4,72,1152]{3,2,1,0:T(8,128)(2,1)}, bf16[4,4,72,4608]{3,2,1,0:T(8,128)(2,1)}, bf16[4,4,288,1152]{3,2,1,0:T(8,128)(2,1)}, f32[2,6912]{1,0:T(2,128)}) custom-call(bf16[4,72,3456]{2,1,0:T(8,128)(2,1)} %bitcast.97, bf16[4,72,1152]{2,1,0:T(8,128)(2,1)} %bitcast.100, bf16[4,72,4608]{2,1,0:T(8,128)(2,1)} %bitcast.89, ...), custom_call_target="tpu_custom_call" | custom-call | tf_op jit(solution)/shard_map/pallas_call | solution.py:433
  158.8 1.6 broadcast_select_fusion.2
  160.3 19.0 %shard_map.136 = (bf16[256,1152]{1,0:T(8,128)(2,1)}, bf16[256,3456]{1,0:T(8,128)(2,1)}, bf16[256,1152]{1,0:T(8,128)(2,1)}, f32[256,1152]{1,0:T(8,128)}, f32[256,...) custom-call(bf16[256,1152]{1,0:T(8,128)(2,1)} %slice_bitcast_fusion., ...), custom_call_target="tpu_custom_call" | custom-call | flops 8455716864 | bytes 47775744 | tf_op jit(solution)/shard_map/pallas_call | solution.py:205
  179.4 3.4 collective-permute-start
  182.8 0.9 slice_bitcast_fusion.1.g_ref
  183.7 12.5 %collective-permute-done = bf16[256,1152]{1,0:T(8,128)(2,1)S(1)} collective-permute-done((bf16[256,1152]{1,0:T(8,128)(2,1)}, bf16[256,1152]{1,0:T(8,128)(2,1)S(1)}, u32[]{:S(2)}, u32[]{:S(2)}) %collective-permute-start) | collective-permute-done | bytes 589856 | tf_op jit(solution)/shard_map/ppermute | solution.py:713
  196.2 0.9 bitcast_select_fusion.1.x_ref
  197.1 18.7 %shard_map.137 = (bf16[256,1152]{1,0:T(8,128)(2,1)}, bf16[256,3456]{1,0:T(8,128)(2,1)}, bf16[256,1152]{1,0:T(8,128)(2,1)}, f32[256,1152]{1,0:T(8,128)}, f32[256,...) custom-call(bf16[256,1152]{1,0:T(8,128)(2,1)} %bitcast_select_fusion, ...), custom_call_target="tpu_custom_call" | custom-call | flops 8455716864 | bytes 47775744 | tf_op jit(solution)/shard_map/pallas_call | solution.py:205
  215.8 4.7 collective-permute-start.2
  220.6 27.6 %shard_map.138 = (f32[1,6912]{1,0:T(1,128)}, bf16[256,1152]{1,0:T(8,128)(2,1)}, bf16[256,4608]{1,0:T(8,128)(2,1)}, bf16[256,1152]{1,0:T(8,128)(2,1)}, bf16[256,3...) custom-call(bf16[256,1152]{1,0:T(8,128)(2,1)} %slice_bitcast_fusion.1.g_ref, ...), custom_call_target="tpu_custom_call" | custom-call | flops 8908701696 | bytes 47775744 | tf_op jit(solution)/shard_map/pallas_call | solution.py:222
  248.2 1.3 collective-permute-start.1
  249.5 0.0 collective-permute-done.2
  249.5 0.9 broadcast_select_fusion.1.x_ref
  250.4 18.6 %shard_map.139 = (bf16[256,1152]{1,0:T(8,128)(2,1)}, bf16[256,3456]{1,0:T(8,128)(2,1)}, bf16[256,1152]{1,0:T(8,128)(2,1)}, f32[256,1152]{1,0:T(8,128)}, f32[256,...) custom-call(bf16[256,1152]{1,0:T(8,128)(2,1)} %broadcast_select_fusi, ...), custom_call_target="tpu_custom_call" | custom-call | flops 8455716864 | bytes 47775744 | tf_op jit(solution)/shard_map/pallas_call | solution.py:205
  269.1 0.0 collective-permute-done.1
  269.1 0.9 bitcast_select_fusion.g_ref
  270.0 27.7 %shard_map.140 = (f32[1,6912]{1,0:T(1,128)}, bf16[256,1152]{1,0:T(8,128)(2,1)}, bf16[256,4608]{1,0:T(8,128)(2,1)}, bf16[256,1152]{1,0:T(8,128)(2,1)}, bf16[256,3...) custom-call(bf16[256,1152]{1,0:T(8,128)(2,1)} %bitcast_select_fusion.g_ref, ...), custom_call_target="tpu_custom_call" | custom-call | flops 8908701696 | bytes 47775744 | tf_op jit(solution)/shard_map/pallas_call | solution.py:222
  297.7 1.4 collective-permute-start.3
  299.2 1.1 copy.16
  300.3 1.1 copy.17
  301.3 1.0 copy.18
  302.4 1.1 copy.20
  303.5 1.1 copy.21
  304.6 1.1 copy.22
  305.6 4.4 copy.19
  310.0 2.4 copy.23
  312.5 1.4 select_bitcast_fusion.1
  313.9 0.7 collective-permute-done.3
  314.6 2.0 broadcast_select_fusion.g_ref
  316.5 27.7 %shard_map.141 = (f32[1,6912]{1,0:T(1,128)}, bf16[256,1152]{1,0:T(8,128)(2,1)}, bf16[256,4608]{1,0:T(8,128)(2,1)}, bf16[256,1152]{1,0:T(8,128)(2,1)}, bf16[256,3...) custom-call(bf16[256,1152]{1,0:T(8,128)(2,1)} %broadcast_select_fusion.g_ref, ...), custom_call_target="tpu_custom_call" | custom-call | flops 8908701696 | bytes 47775744 | tf_op jit(solution)/shard_map/pallas_call | solution.py:222
  344.3 0.0 copy-start.15
  344.3 196.7 %shard_map.142 = (bf16[4,72,3456]{2,1,0:T(8,128)(2,1)}, bf16[4,72,1152]{2,1,0:T(8,128)(2,1)}, bf16[4,72,4608]{2,1,0:T(8,128)(2,1)}, bf16[4,4,72,1152]{3,2,1,0:T(...) custom-call(bf16[4,288,256]{2,1,0:T(8,128)(2,1)} %bitcast.104, bf16[4,288,256]{2,1,0:T(8,128)(2,1)} %bitcast.105, ...), custom_call_target="tpu_custom_call" | custom-call | flops 16307453952 | bytes 28311552 | tf_op jit(solution)/shard_map/pallas_call | solution.py:654
  541.0 0.7 copy.24
  541.7 0.1 reshape.121
  541.8 0.6 fusion.7
  542.4 0.9 slice.35
  543.3 2.2 bitcast_convert_fusion.2
  545.6 2.2 bitcast_convert_fusion.1
  547.8 0.8 copy-done.1
  548.6 3.0 bitcast_convert_fusion
  551.7 2.7 convert.7
  554.4 0.1 select_bitcast_fusion
  554.5 1.6 maximum_bitcast_fusion
  556.1 4.5 convolution_bitcast_fusion
  (32 shorter events, 0.1 us)
Async XLA Ops:
  1.4 157.4 %copy-start.16 = (bf16[2,1152]{1,0:T(2,128)(2,1)}, bf16[2,1152]{1,0:T(2,128)(2,1)S(1)}, u32[]{:S(2)}) copy-start(bf16[2,1152]{1,0:T(2,128)(2,1)S(1)} %fusion.5.refs_18_) | copy-start | bytes 13828
  160.3 22.5 %copy-start.3 = (bf16[2,256,1152]{2,1,0:T(8,128)(2,1)S(1)}, bf16[2,256,1152]{2,1,0:T(8,128)(2,1)}, u32[]{:S(2)}) copy-start(bf16[2,256,1152]{2,1,0:T(8,128)(2,1)} %param.15) | copy-start | bytes 3538948
  160.3 35.9 %copy-start.2 = (bf16[2,256,1152]{2,1,0:T(8,128)(2,1)S(1)}, bf16[2,256,1152]{2,1,0:T(8,128)(2,1)}, u32[]{:S(2)}) copy-start(bf16[2,256,1152]{2,1,0:T(8,128)(2,1)} %param.8) | copy-start | bytes 3538948
  179.4 16.8 %collective-permute-start = (bf16[256,1152]{1,0:T(8,128)(2,1)}, bf16[256,1152]{1,0:T(8,128)(2,1)S(1)}, u32[]{:S(2)}, u32[]{:S(2)}) collective-permute-start(bf16[256,1152]{1,0:T(8,128)(2,1)} %get-tuple-element.68), channel_id=1, source_target_pairs={{0,16},{1,17},{2,18},{3,19},{4,20},{5,21},{6,22},{7,23},{8,24},{9,... | collective-permute-start | bytes 1769480 | tf_op jit(solution)/shard_map/ppermute | solution.py:713
  215.8 33.7 %collective-permute-start.2 = (bf16[256,1152]{1,0:T(8,128)(2,1)}, bf16[256,1152]{1,0:T(8,128)(2,1)S(1)}, u32[]{:S(2)}, u32[]{:S(2)}) collective-permute-start(bf16[256,1152]{1,0:T(8,128)(2,1)} %get-tuple-element.75), channel_id=1, source_target_pairs={{0,16},{1,17},{2,18},{3,19},{4,20},{5,21},{6,22},{7,23},{8,24},{9,... | collective-permute-start | bytes 1769480 | tf_op jit(solution)/shard_map/ppermute | solution.py:716
  248.2 20.9 %collective-permute-start.1 = (bf16[256,1152]{1,0:T(8,128)(2,1)}, bf16[256,1152]{1,0:T(8,128)(2,1)S(1)}, u32[]{:S(2)}, u32[]{:S(2)}) collective-permute-start(bf16[256,1152]{1,0:T(8,128)(2,1)} %get-tuple-element.74), channel_id=1, source_target_pairs={{16,0},{17,1},{18,2},{19,3},{20,4},{21,5},{22,6},{23,7},{24,8},{25... | collective-permute-start | bytes 1769480 | tf_op jit(solution)/shard_map/ppermute | solution.py:718
  270.0 29.2 %copy-start.13 = (bf16[256,1152]{1,0:T(8,128)(2,1)S(1)}, bf16[256,1152]{1,0:T(8,128)(2,1)}, u32[]{:S(2)}) copy-start(bf16[256,1152]{1,0:T(8,128)(2,1)} %get-tuple-element.95) | copy-start | bytes 1769476
  270.0 30.3 %copy-start.12 = (bf16[256,1152]{1,0:T(8,128)(2,1)S(1)}, bf16[256,1152]{1,0:T(8,128)(2,1)}, u32[]{:S(2)}) copy-start(bf16[256,1152]{1,0:T(8,128)(2,1)} %get-tuple-element.96) | copy-start | bytes 1769476
  297.7 3.6 copy-start.11
  297.7 16.8 %collective-permute-start.3 = (bf16[256,1152]{1,0:T(8,128)(2,1)}, bf16[256,1152]{1,0:T(8,128)(2,1)}, u32[]{:S(2)}, u32[]{:S(2)}) collective-permute-start(bf16[256,1152]{1,0:T(8,128)(2,1)} %get-tuple-element.84), channel_id=1, source_target_pairs={{16,0},{17,1},{18,2},{19,3},{20,4},{21,5},{22,6},{23,7},{24,8},{25... | collective-permute-start | bytes 1769480 | tf_op jit(solution)/shard_map/ppermute | solution.py:726
  299.2 3.2 copy-start.10
  300.3 3.2 copy-start.9
  301.3 3.2 copy-start.8
  305.6 4.4 copy-start.4
  344.3 197.5 %copy-start.15 = (bf16[2,1152]{1,0:T(2,128)(2,1)S(1)}, bf16[2,1152]{1,0:T(2,128)(2,1)}, u32[]{:S(2)}) copy-start(bf16[2,1152]{1,0:T(2,128)(2,1)} %param.9) | copy-start | bytes 13828
  541.8 3.8 copy-start.5
  545.6 3.1 copy-start.1
  548.6 3.0 copy-start
  551.7 2.7 copy-start.6
  551.7 2.7 copy-start.7
  554.5 1.6 copy-start.14

commit v3 on v2

--- a/solution.py
+++ b/solution.py
@@ -90,16 +90,28 @@
         wqkv_v,wout_v,w1_v,w2_v,first_v,project_v,att_v,branch_v,middle_v,second_v,u_v,h_v,f_v,y_v,y_low_v,in_sems,out_sems):
     width=wqkv_v.shape[2]; group=w1_v.shape[2]
     come=Copies(in_sems); leave=Copies(out_sems)
-    project_in=[come.start(wqkv.at[:,i*width:(i+1)*width],wqkv_v.at[i]) for i in range(3)]
+    third=lambda i: pl.ds(pl.multiple_of(i*width,128),width)
+    part_of=lambda i: pl.ds(pl.multiple_of(i*group,128),group)
+    def project_copy(i): return pltpu.make_async_copy(wqkv.at[:,third(i)],wqkv_v.at[i],in_sems.at[1+i])
+    def feed_copies(i):
+        return (pltpu.make_async_copy(w1.at[:,part_of(i)],w1_v.at[i],in_sems.at[4+2*i]),
+            pltpu.make_async_copy(w2.at[part_of(i)],w2_v.at[i],in_sems.at[5+2*i]))
+    def feed_leave(i):
+        return (pltpu.make_async_copy(u_v.at[i],u_out.at[:,part_of(i)],out_sems.at[9+2*i]),
+            pltpu.make_async_copy(h_v.at[i],h_out.at[:,part_of(i)],out_sems.at[10+2*i]))
+    for i in range(3): project_copy(i).start()
     out_in=come.start(wout,wout_v)
-    feed_in=[(come.start(w1.at[:,i*group:(i+1)*group],w1_v.at[i]),come.start(w2.at[i*group:(i+1)*group],w2_v.at[i])) for i in range(FEED_GROUPS)]
+    for i in range(FEED_GROUPS):
+        for copy in feed_copies(i): copy.start()
     shift_one,scale_one,gate_one,shift_two,scale_two,gate_two=(mod_ref[:,i*D:(i+1)*D] for i in range(6))
     x=x_ref[...].astype(jnp.float32)
     first_v[...]=(center_scale(x)[0]*(1.0+scale_one)+shift_one).astype(low)
     leave.start(first_v,first_out)
-    for i in range(3):
-        project_in[i].wait()
-        project_v[:,i*width:(i+1)*width]=dot(first_v[...],wqkv_v[i]).astype(low)
+    def project_part(i,carry):
+        project_copy(i).wait()
+        project_v[:,third(i)]=dot(first_v[...],wqkv_v[i]).astype(low)
+        return carry
+    lax.fori_loop(0,3,project_part,0)
     leave.start(project_v,project_out)
     attention_kernel(project_v,att_v)
     leave.start(att_v,att_out)
@@ -112,21 +124,21 @@
     leave.start(middle_v,middle_out)
     second_v[...]=(center_scale(middle)[0]*(1.0+scale_two)+shift_two).astype(low)
     leave.start(second_v,second_out)
-    for i in range(FEED_GROUPS):
-        for copy in feed_in[i]: copy.wait()
+    f_v[...]=jnp.zeros_like(f_v)
+    def feed_part(i,carry):
+        for copy in feed_copies(i): copy.wait()
         prev=None
         def back(p,u):
             h=act_of(u); h_v[i,:,p]=h
-            part=dot(h,w2_v[i,p,:])
-            if i==0 and p.start==0: f_v[...]=part
-            else: f_v[...]+=part
+            f_v[...]+=dot(h,w2_v[i,p,:])
         for p in chunks_of(group):
             u=dot(second_v[...],w1_v[i,:,p]); u_v[i,:,p]=u
             if prev is not None: back(*prev)
             prev=(p,u)
         back(*prev)
-        leave.start(u_v.at[i],u_out.at[:,i*group:(i+1)*group])
-        leave.start(h_v.at[i],h_out.at[:,i*group:(i+1)*group])
+        for copy in feed_leave(i): copy.start()
+        return carry
+    lax.fori_loop(0,FEED_GROUPS,feed_part,0)
     y=middle_v[...]+gate_two*f_v[...]
     y_v[...]=y
     y_low_v[...]=y.astype(low)
@@ -134,16 +146,22 @@
     leave.start(f_v,f_out)
     leave.start(y_v,y_out)
     leave.wait_all()
+    for i in range(FEED_GROUPS):
+        for copy in feed_leave(i): copy.wait()
 
 def backward_kernel(g_ref,mod_ref,x_ref,feed_out,middle,branch,u,project,wqkv,wout,w1,w2,
         mod_out,df_out,du_out,do_out,dproject_out,dx_out,dx_low_out,
         feed_v,middle_v,branch_v,u_v,project_v,wqkv_v,wout_v,w1_v,w2_v,df_v,du_v,do_v,datt_v,dproject_v,acc_v,dx_v,dx_low_v,in_sems,out_sems):
     group=w1_v.shape[2]
     come=Copies(in_sems); leave=Copies(out_sems)
-    feed_in=[]
+    part_of=lambda i: pl.ds(pl.multiple_of(i*group,128),group)
+    def feed_copies(i):
+        return (pltpu.make_async_copy(w2.at[part_of(i)],w2_v.at[i],in_sems.at[6+3*i]),
+            pltpu.make_async_copy(u.at[:,part_of(i)],u_v.at[i],in_sems.at[7+3*i]),
+            pltpu.make_async_copy(w1.at[:,part_of(i)],w1_v.at[i],in_sems.at[8+3*i]))
+    def feed_leave(i): return pltpu.make_async_copy(du_v.at[i],du_out.at[:,part_of(i)],out_sems.at[5+i])
     for i in range(FEED_GROUPS):
-        feed_in.append((come.start(w2.at[i*group:(i+1)*group],w2_v.at[i]),come.start(u.at[:,i*group:(i+1)*group],u_v.at[i]),
-            come.start(w1.at[:,i*group:(i+1)*group],w1_v.at[i])))
+        for copy in feed_copies(i): copy.start()
         if i==0: feed_copy=come.start(feed_out,feed_v)
     middle_in=come.start(middle,middle_v); branch_in=come.start(branch,branch_v)
     out_in=come.start(wout,wout_v); project_in=come.start(project,project_v); qkv_in=come.start(wqkv,wqkv_v)
@@ -151,20 +169,21 @@
     total=lambda values: jnp.sum(values,axis=0,keepdims=True)
     df_v[...]=(gate_two*g_ref[...].astype(jnp.float32)).astype(low)
     leave.start(df_v,df_out)
-    for i in range(FEED_GROUPS):
-        for copy in feed_in[i]: copy.wait()
+    acc_v[...]=jnp.zeros_like(acc_v)
+    def feed_part(i,carry):
+        for copy in feed_copies(i): copy.wait()
         prev=None
         def back(p,dh):
             du=(dh*slope_of(u_v[i,:,p])).astype(low); du_v[i,:,p]=du
-            part=dot(du,w1_v[i,:,p],NT)
-            if i==0 and p.start==0: acc_v[...]=part
-            else: acc_v[...]+=part
+            acc_v[...]+=dot(du,w1_v[i,:,p],NT)
         for p in chunks_of(group):
             dh=dot(df_v[...],w2_v[i,p,:],NT)
             if prev is not None: back(*prev)
             prev=(p,dh)
         back(*prev)
-        leave.start(du_v.at[i],du_out.at[:,i*group:(i+1)*group])
+        feed_leave(i).start()
+        return carry
+    lax.fori_loop(0,FEED_GROUPS,feed_part,0)
     feed_copy.wait(); middle_in.wait(); branch_in.wait()
     g=g_ref[...].astype(jnp.float32)
     mod_out[:,5*D:6*D]=total(g*feed_v[...])
@@ -193,6 +212,7 @@
     leave.start(dx_low_v,dx_low_out)
     leave.start(dx_v,dx_out)
     leave.wait_all()
+    for i in range(FEED_GROUPS): feed_leave(i).wait()
 
 LAYER_VMEM=60 * 1024 * 1024
 def forward_layer(x,mod,weights):

time: 572 us -> 570 us (level)
  no operation moved by 1% of the time
where the time goes in v3:
time: 570 us; the launch traced here: 561 us
  Pallas kernels  492 us (86%)
  other arithmetic  20.8 us (4%)
  local copies, waits for them, and re-layouts  19.3 us (3%)
  waiting for transfers between devices  12.7 us (2%)
  starting transfers between devices  10.9 us (2%)
    pallas_call x1, Pallas kernels, reduce_all(): pl.pallas_call(functools.partial(reduce_kernel, blocks), in_specs=[any_]...  196 us
    pallas_call x1, Pallas kernels, gather_all(): pl.pallas_call(functools.partial(gather_kernel, shards, reps, arrays, chu...  155 us
    pallas_call x3, Pallas kernels, backward_layer(): pl.pallas_call(backward_kernel, in_specs=[inside] * 3 + [any_] * 9, out_s...  82.8 us
    pallas_call x3, Pallas kernels, forward_layer(): pl.pallas_call(forward_kernel, in_specs=[inside, inside] + [any_] * 4, ou...  57.5 us
    ppermute x2, waiting for transfers between devices, body(): incoming = lax.ppermute(sent, 'section', forth)  12 us
  transfers between devices with their start and end apart: 4, of which 2 were waited for; matrix products, arithmetic and copies ran while one was open for 3% of the time, Pallas kernels for 8%

profile of v3, /device:TPU:0, one launch (start us, length us, event | category | flops | bytes accessed | tf_op | source)
XLA Modules:
  0.0 561.0 jit_solution(16970327042206837922)
XLA Ops:
  0.6 0.7 fusion.5.refs_18_
  1.4 0.1 reshape.108
  1.5 0.6 copy.26
  2.1 1.9 slice_bitcast_fusion.x_ref
  4.0 154.8 %shard_map.135 = (bf16[4,4,72,3456]{3,2,1,0:T(8,128)(2,1)}, bf16[4,4,72,1152]{3,2,1,0:T(8,128)(2,1)}, bf16[4,4,72,4608]{3,2,1,0:T(8,128)(2,1)}, bf16[4,4,288,1152]{3,2,1,0:T(8,128)(2,1)}, f32[2,6912]{1,0:T(2,128)}) custom-call(bf16[4,72,3456]{2,1,0:T(8,128)(2,1)} %bitcast.97, bf16[4,72,1152]{2,1,0:T(8,128)(2,1)} %bitcast.100, bf16[4,72,4608]{2,1,0:T(8,128)(2,1)} %bitcast.89, ...), custom_call_target="tpu_custom_call" | custom-call | tf_op jit(solution)/shard_map/pallas_call | solution.py:453
  158.8 1.6 broadcast_select_fusion.2
  160.3 19.3 %shard_map.136 = (bf16[256,1152]{1,0:T(8,128)(2,1)}, bf16[256,3456]{1,0:T(8,128)(2,1)}, bf16[256,1152]{1,0:T(8,128)(2,1)}, f32[256,1152]{1,0:T(8,128)}, f32[256,...) custom-call(bf16[256,1152]{1,0:T(8,128)(2,1)} %slice_bitcast_fusion., ...), custom_call_target="tpu_custom_call" | custom-call | flops 8455716864 | bytes 47775744 | tf_op jit(solution)/shard_map/pallas_call | solution.py:225
  179.6 3.9 collective-permute-start
  183.5 0.9 slice_bitcast_fusion.1.g_ref
  184.4 12.0 %collective-permute-done = bf16[256,1152]{1,0:T(8,128)(2,1)S(1)} collective-permute-done((bf16[256,1152]{1,0:T(8,128)(2,1)}, bf16[256,1152]{1,0:T(8,128)(2,1)S(1)}, u32[]{:S(2)}, u32[]{:S(2)}) %collective-permute-start) | collective-permute-done | bytes 589856 | tf_op jit(solution)/shard_map/ppermute | solution.py:733
  196.5 0.9 bitcast_select_fusion.1.x_ref
  197.4 19.2 %shard_map.137 = (bf16[256,1152]{1,0:T(8,128)(2,1)}, bf16[256,3456]{1,0:T(8,128)(2,1)}, bf16[256,1152]{1,0:T(8,128)(2,1)}, f32[256,1152]{1,0:T(8,128)}, f32[256,...) custom-call(bf16[256,1152]{1,0:T(8,128)(2,1)} %bitcast_select_fusion, ...), custom_call_target="tpu_custom_call" | custom-call | flops 8455716864 | bytes 47775744 | tf_op jit(solution)/shard_map/pallas_call | solution.py:225
  216.5 4.3 collective-permute-start.2
  220.8 27.5 %shard_map.138 = (f32[1,6912]{1,0:T(1,128)}, bf16[256,1152]{1,0:T(8,128)(2,1)}, bf16[256,4608]{1,0:T(8,128)(2,1)}, bf16[256,1152]{1,0:T(8,128)(2,1)}, bf16[256,3...) custom-call(bf16[256,1152]{1,0:T(8,128)(2,1)} %slice_bitcast_fusion.1.g_ref, ...), custom_call_target="tpu_custom_call" | custom-call | flops 8908701696 | bytes 47775744 | tf_op jit(solution)/shard_map/pallas_call | solution.py:242
  248.3 1.3 collective-permute-start.1
  249.6 0.0 collective-permute-done.2
  249.6 0.9 broadcast_select_fusion.1.x_ref
  250.5 19.1 %shard_map.139 = (bf16[256,1152]{1,0:T(8,128)(2,1)}, bf16[256,3456]{1,0:T(8,128)(2,1)}, bf16[256,1152]{1,0:T(8,128)(2,1)}, f32[256,1152]{1,0:T(8,128)}, f32[256,...) custom-call(bf16[256,1152]{1,0:T(8,128)(2,1)} %broadcast_select_fusi, ...), custom_call_target="tpu_custom_call" | custom-call | flops 8455716864 | bytes 47775744 | tf_op jit(solution)/shard_map/pallas_call | solution.py:225
  269.6 0.0 collective-permute-done.1
  269.6 0.9 bitcast_select_fusion.g_ref
  270.5 27.8 %shard_map.140 = (f32[1,6912]{1,0:T(1,128)}, bf16[256,1152]{1,0:T(8,128)(2,1)}, bf16[256,4608]{1,0:T(8,128)(2,1)}, bf16[256,1152]{1,0:T(8,128)(2,1)}, bf16[256,3...) custom-call(bf16[256,1152]{1,0:T(8,128)(2,1)} %bitcast_select_fusion.g_ref, ...), custom_call_target="tpu_custom_call" | custom-call | flops 8908701696 | bytes 47775744 | tf_op jit(solution)/shard_map/pallas_call | solution.py:242
  298.3 1.4 collective-permute-start.3
  299.8 1.1 copy.16
  300.9 1.1 copy.17
  301.9 1.0 copy.18
  303.0 1.1 copy.20
  304.1 1.1 copy.21
  305.2 1.1 copy.22
  306.2 4.4 copy.19
  310.6 2.4 copy.23
  313.1 1.4 select_bitcast_fusion.1
  314.5 0.7 collective-permute-done.3
  315.2 2.0 broadcast_select_fusion.g_ref
  317.1 27.5 %shard_map.141 = (f32[1,6912]{1,0:T(1,128)}, bf16[256,1152]{1,0:T(8,128)(2,1)}, bf16[256,4608]{1,0:T(8,128)(2,1)}, bf16[256,1152]{1,0:T(8,128)(2,1)}, bf16[256,3...) custom-call(bf16[256,1152]{1,0:T(8,128)(2,1)} %broadcast_select_fusion.g_ref, ...), custom_call_target="tpu_custom_call" | custom-call | flops 8908701696 | bytes 47775744 | tf_op jit(solution)/shard_map/pallas_call | solution.py:242
  344.6 0.0 copy-start.15
  344.7 196.5 %shard_map.142 = (bf16[4,72,3456]{2,1,0:T(8,128)(2,1)}, bf16[4,72,1152]{2,1,0:T(8,128)(2,1)}, bf16[4,72,4608]{2,1,0:T(8,128)(2,1)}, bf16[4,4,72,1152]{3,2,1,0:T(...) custom-call(bf16[4,288,256]{2,1,0:T(8,128)(2,1)} %bitcast.104, bf16[4,288,256]{2,1,0:T(8,128)(2,1)} %bitcast.105, ...), custom_call_target="tpu_custom_call" | custom-call | flops 16307453952 | bytes 28311552 | tf_op jit(solution)/shard_map/pallas_call | solution.py:674
  541.1 0.7 copy.24
  541.9 0.1 reshape.121
  542.0 0.6 fusion.7
  542.6 0.9 slice.35
  543.5 2.2 bitcast_convert_fusion.2
  545.7 2.2 bitcast_convert_fusion.1
  548.0 0.8 copy-done.1
  548.8 3.0 bitcast_convert_fusion
  551.8 2.7 convert.7
  554.5 0.1 select_bitcast_fusion
  554.7 1.6 maximum_bitcast_fusion
  556.2 4.5 convolution_bitcast_fusion
  (32 shorter events, 0.1 us)
Async XLA Ops:
  1.4 157.4 %copy-start.16 = (bf16[2,1152]{1,0:T(2,128)(2,1)}, bf16[2,1152]{1,0:T(2,128)(2,1)S(1)}, u32[]{:S(2)}) copy-start(bf16[2,1152]{1,0:T(2,128)(2,1)S(1)} %fusion.5.refs_18_) | copy-start | bytes 13828
  160.3 23.2 %copy-start.3 = (bf16[2,256,1152]{2,1,0:T(8,128)(2,1)S(1)}, bf16[2,256,1152]{2,1,0:T(8,128)(2,1)}, u32[]{:S(2)}) copy-start(bf16[2,256,1152]{2,1,0:T(8,128)(2,1)} %param.15) | copy-start | bytes 3538948
  160.3 36.1 %copy-start.2 = (bf16[2,256,1152]{2,1,0:T(8,128)(2,1)S(1)}, bf16[2,256,1152]{2,1,0:T(8,128)(2,1)}, u32[]{:S(2)}) copy-start(bf16[2,256,1152]{2,1,0:T(8,128)(2,1)} %param.8) | copy-start | bytes 3538948
  179.6 16.8 %collective-permute-start = (bf16[256,1152]{1,0:T(8,128)(2,1)}, bf16[256,1152]{1,0:T(8,128)(2,1)S(1)}, u32[]{:S(2)}, u32[]{:S(2)}) collective-permute-start(bf16[256,1152]{1,0:T(8,128)(2,1)} %get-tuple-element.68), channel_id=1, source_target_pairs={{0,16},{1,17},{2,18},{3,19},{4,20},{5,21},{6,22},{7,23},{8,24},{9,... | collective-permute-start | bytes 1769480 | tf_op jit(solution)/shard_map/ppermute | solution.py:733
  216.5 33.1 %collective-permute-start.2 = (bf16[256,1152]{1,0:T(8,128)(2,1)}, bf16[256,1152]{1,0:T(8,128)(2,1)S(1)}, u32[]{:S(2)}, u32[]{:S(2)}) collective-permute-start(bf16[256,1152]{1,0:T(8,128)(2,1)} %get-tuple-element.75), channel_id=1, source_target_pairs={{0,16},{1,17},{2,18},{3,19},{4,20},{5,21},{6,22},{7,23},{8,24},{9,... | collective-permute-start | bytes 1769480 | tf_op jit(solution)/shard_map/ppermute | solution.py:736
  248.3 21.3 %collective-permute-start.1 = (bf16[256,1152]{1,0:T(8,128)(2,1)}, bf16[256,1152]{1,0:T(8,128)(2,1)S(1)}, u32[]{:S(2)}, u32[]{:S(2)}) collective-permute-start(bf16[256,1152]{1,0:T(8,128)(2,1)} %get-tuple-element.74), channel_id=1, source_target_pairs={{16,0},{17,1},{18,2},{19,3},{20,4},{21,5},{22,6},{23,7},{24,8},{25... | collective-permute-start | bytes 1769480 | tf_op jit(solution)/shard_map/ppermute | solution.py:738
  270.5 29.2 %copy-start.13 = (bf16[256,1152]{1,0:T(8,128)(2,1)S(1)}, bf16[256,1152]{1,0:T(8,128)(2,1)}, u32[]{:S(2)}) copy-start(bf16[256,1152]{1,0:T(8,128)(2,1)} %get-tuple-element.95) | copy-start | bytes 1769476
  270.5 30.3 %copy-start.12 = (bf16[256,1152]{1,0:T(8,128)(2,1)S(1)}, bf16[256,1152]{1,0:T(8,128)(2,1)}, u32[]{:S(2)}) copy-start(bf16[256,1152]{1,0:T(8,128)(2,1)} %get-tuple-element.96) | copy-start | bytes 1769476
  298.3 3.6 copy-start.11
  298.3 16.8 %collective-permute-start.3 = (bf16[256,1152]{1,0:T(8,128)(2,1)}, bf16[256,1152]{1,0:T(8,128)(2,1)}, u32[]{:S(2)}, u32[]{:S(2)}) collective-permute-start(bf16[256,1152]{1,0:T(8,128)(2,1)} %get-tuple-element.84), channel_id=1, source_target_pairs={{16,0},{17,1},{18,2},{19,3},{20,4},{21,5},{22,6},{23,7},{24,8},{25... | collective-permute-start | bytes 1769480 | tf_op jit(solution)/shard_map/ppermute | solution.py:746
  299.8 3.2 copy-start.10
  300.9 3.2 copy-start.9
  301.9 3.2 copy-start.8
  306.2 4.4 copy-start.4
  344.6 197.3 %copy-start.15 = (bf16[2,1152]{1,0:T(2,128)(2,1)S(1)}, bf16[2,1152]{1,0:T(2,128)(2,1)}, u32[]{:S(2)}) copy-start(bf16[2,1152]{1,0:T(2,128)(2,1)} %param.9) | copy-start | bytes 13828
  542.0 3.8 copy-start.5
  545.7 3.1 copy-start.1
  548.8 3.0 copy-start
  551.8 2.7 copy-start.6
  551.8 2.7 copy-start.7
  554.7 1.6 copy-start.14

commit v4 on v3

--- a/solution.py
+++ b/solution.py
@@ -76,6 +76,9 @@
     return (grad-mean_grad-normed*mean_dot)*scale
 def chunks_of(span): return [slice(a,a+FEED_CHUNK) for a in range(0,span,FEED_CHUNK)]
 
+def by_section(zero,one):
+    return jnp.where(lax.axis_index("section")==0,zero,one)
+
 class Copies:
     def __init__(self,sems): self.sems=sems; self.made=[]
     def start(self,src,dst):
@@ -85,10 +88,11 @@
     def wait_all(self):
         for copy in self.made: copy.wait()
 
-def forward_kernel(x_ref,mod_ref,wqkv,wout,w1,w2,
+def forward_kernel(rows,places,x_zero,x_one,mod_ref,wqkv,wout,w1,w2,
         first_out,project_out,att_out,branch_out,middle_out,second_out,u_out,h_out,f_out,y_out,y_low_out,
         wqkv_v,wout_v,w1_v,w2_v,first_v,project_v,att_v,branch_v,middle_v,second_v,u_v,h_v,f_v,y_v,y_low_v,in_sems,out_sems):
     width=wqkv_v.shape[2]; group=w1_v.shape[2]
+    x_zero,x_one=at_latent((x_zero,x_one),places)
     come=Copies(in_sems); leave=Copies(out_sems)
     third=lambda i: pl.ds(pl.multiple_of(i*width,128),width)
     part_of=lambda i: pl.ds(pl.multiple_of(i*group,128),group)
@@ -103,8 +107,9 @@
     out_in=come.start(wout,wout_v)
     for i in range(FEED_GROUPS):
         for copy in feed_copies(i): copy.start()
-    shift_one,scale_one,gate_one,shift_two,scale_two,gate_two=(mod_ref[:,i*D:(i+1)*D] for i in range(6))
-    x=x_ref[...].astype(jnp.float32)
+    shift_one,scale_one,gate_one,shift_two,scale_two,gate_two=(
+        by_section(mod_ref[rows[0]:rows[0]+1,i*D:(i+1)*D],mod_ref[rows[1]:rows[1]+1,i*D:(i+1)*D]) for i in range(6))
+    x=by_section(x_zero[...],x_one[...]).astype(jnp.float32)
     first_v[...]=(center_scale(x)[0]*(1.0+scale_one)+shift_one).astype(low)
     leave.start(first_v,first_out)
     def project_part(i,carry):
@@ -119,7 +124,7 @@
     branch=dot(att_v[...],wout_v[...])
     branch_v[...]=branch
     leave.start(branch_v,branch_out)
-    middle=x_ref[...].astype(jnp.float32)+gate_one*branch
+    middle=by_section(x_zero[...],x_one[...]).astype(jnp.float32)+gate_one*branch
     middle_v[...]=middle
     leave.start(middle_v,middle_out)
     second_v[...]=(center_scale(middle)[0]*(1.0+scale_two)+shift_two).astype(low)
@@ -149,9 +154,10 @@
     for i in range(FEED_GROUPS):
         for copy in feed_leave(i): copy.wait()
 
-def backward_kernel(g_ref,mod_ref,x_ref,feed_out,middle,branch,u,project,wqkv,wout,w1,w2,
+def backward_kernel(rows,places,g_zero,g_one,mod_ref,x_zero,x_one,feed_out,middle,branch,u,project,wqkv,wout,w1,w2,
         mod_out,df_out,du_out,do_out,dproject_out,dx_out,dx_low_out,
         feed_v,middle_v,branch_v,u_v,project_v,wqkv_v,wout_v,w1_v,w2_v,df_v,du_v,do_v,datt_v,dproject_v,acc_v,dx_v,dx_low_v,in_sems,out_sems):
+    g_zero,g_one,x_zero,x_one=at_latent((g_zero,g_one,x_zero,x_one),places)
     group=w1_v.shape[2]
     come=Copies(in_sems); leave=Copies(out_sems)
     part_of=lambda i: pl.ds(pl.multiple_of(i*group,128),group)
@@ -165,9 +171,10 @@
         if i==0: feed_copy=come.start(feed_out,feed_v)
     middle_in=come.start(middle,middle_v); branch_in=come.start(branch,branch_v)
     out_in=come.start(wout,wout_v); project_in=come.start(project,project_v); qkv_in=come.start(wqkv,wqkv_v)
-    _,scale_one,gate_one,_,scale_two,gate_two=(mod_ref[:,i*D:(i+1)*D] for i in range(6))
+    _,scale_one,gate_one,_,scale_two,gate_two=(
+        by_section(mod_ref[rows[0]:rows[0]+1,i*D:(i+1)*D],mod_ref[rows[1]:rows[1]+1,i*D:(i+1)*D]) for i in range(6))
     total=lambda values: jnp.sum(values,axis=0,keepdims=True)
-    df_v[...]=(gate_two*g_ref[...].astype(jnp.float32)).astype(low)
+    df_v[...]=(gate_two*by_section(g_zero[...],g_one[...]).astype(jnp.float32)).astype(low)
     leave.start(df_v,df_out)
     acc_v[...]=jnp.zeros_like(acc_v)
     def feed_part(i,carry):
@@ -185,7 +192,7 @@
         return carry
     lax.fori_loop(0,FEED_GROUPS,feed_part,0)
     feed_copy.wait(); middle_in.wait(); branch_in.wait()
-    g=g_ref[...].astype(jnp.float32)
+    g=by_section(g_zero[...],g_one[...]).astype(jnp.float32)
     mod_out[:,5*D:6*D]=total(g*feed_v[...])
     dh=acc_v[...]
     normed,inverse=center_scale(middle_v[...])
@@ -203,7 +210,7 @@
     leave.start(dproject_v,dproject_out)
     qkv_in.wait()
     dh=dot(dproject_v[...],wqkv_v[...],NT)
-    normed,inverse=center_scale(x_ref[...].astype(jnp.float32))
+    normed,inverse=center_scale(by_section(x_zero[...],x_one[...]).astype(jnp.float32))
     mod_out[:,0*D:1*D]=total(dh)
     mod_out[:,1*D:2*D]=total(dh*normed)
     dx=dx_v[...]+norm_back(normed,inverse,dh*(1.0+scale_one))
@@ -215,14 +222,19 @@
     for i in range(FEED_GROUPS): feed_leave(i).wait()
 
 LAYER_VMEM=60 * 1024 * 1024
-def forward_layer(x,mod,weights):
+def one_latent(source):
+    return source if isinstance(source,tuple) else (source,None)
+def at_latent(refs,places):
+    return [ref if place is None else ref.at[place] for ref,place in zip(refs,places)]
+def forward_layer(inputs,mod,rows,weights):
     _,_,w1,_=weights
-    t,d=x.shape; ff=w1.shape[1]; group=ff//FEED_GROUPS
+    operands,places=zip(*(one_latent(source) for source in inputs))
+    t,d=operands[0].shape[-2:]; ff=w1.shape[1]; group=ff//FEED_GROUPS
     made=lambda width,dtype: jax.ShapeDtypeStruct((t,width),dtype)
     f32=jnp.float32
     v=pltpu.VMEM
     any_=pl.BlockSpec(memory_space=pl.ANY); inside=pl.BlockSpec(memory_space=pltpu.VMEM)
-    return pl.pallas_call(forward_kernel,in_specs=[inside,inside]+[any_]*4,out_specs=[any_]*11,
+    return pl.pallas_call(functools.partial(forward_kernel,rows,places),in_specs=[inside]*3+[any_]*4,out_specs=[any_]*11,
         out_shape=[made(d,low),made(3*d,low),made(d,low),made(d,f32),made(d,f32),made(d,low),made(ff,f32),made(ff,low),made(d,f32),made(d,f32),made(d,low)],
         scratch_shapes=[v((3,d,d),low),v((d,d),low),v((FEED_GROUPS,d,group),low),v((FEED_GROUPS,group,d),low),
             v((t,d),low),v((t,3*d),low),v((t,d),low),v((t,d),f32),v((t,d),f32),v((t,d),low),
@@ -230,16 +242,17 @@
             pltpu.SemaphoreType.DMA((4+2*FEED_GROUPS,)),pltpu.SemaphoreType.DMA((9+2*FEED_GROUPS,))],
         compiler_params=pltpu.CompilerParams(vmem_limit_bytes=LAYER_VMEM),
         cost_estimate=pl.CostEstimate(flops=2*t*d*(4*d+2*ff)+4*t*t*d,bytes_accessed=2*d*(4*d+2*ff)+t*(30*d+6*ff),transcendentals=t*(ff+HEADS*t)),
-        )(x,mod,*weights)
-def backward_layer(g,mod,x,kept,weights):
+        )(*operands,mod,*weights)
+def backward_layer(grads,mod,rows,inputs,kept,weights):
     _,project,_,branch,middle,_,u,_,feed_out=kept
     _,_,w1,_=weights
-    t,d=x.shape; ff=w1.shape[1]; group=ff//FEED_GROUPS
+    operands,places=zip(*(one_latent(source) for source in (*grads,*inputs)))
+    t,d=operands[2].shape[-2:]; ff=w1.shape[1]; group=ff//FEED_GROUPS
     made=lambda width,dtype: jax.ShapeDtypeStruct((t,width),dtype)
     f32=jnp.float32
     v=pltpu.VMEM
     any_=pl.BlockSpec(memory_space=pl.ANY); inside=pl.BlockSpec(memory_space=pltpu.VMEM)
-    return pl.pallas_call(backward_kernel,in_specs=[inside]*3+[any_]*9,out_specs=[inside]+[any_]*6,
+    return pl.pallas_call(functools.partial(backward_kernel,rows,places),in_specs=[inside]*5+[any_]*9,out_specs=[inside]+[any_]*6,
         out_shape=[jax.ShapeDtypeStruct((1,6*d),f32),made(d,low),made(ff,low),made(d,low),made(3*d,low),made(d,f32),made(d,low)],
         scratch_shapes=[v((t,d),f32),v((t,d),f32),v((t,d),f32),v((FEED_GROUPS,t,group),f32),v((t,3*d),low),
             v((d,3*d),low),v((d,d),low),v((FEED_GROUPS,d,group),low),v((FEED_GROUPS,group,d),low),
@@ -247,7 +260,7 @@
             pltpu.SemaphoreType.DMA((6+3*FEED_GROUPS,)),pltpu.SemaphoreType.DMA((5+FEED_GROUPS,))],
         compiler_params=pltpu.CompilerParams(vmem_limit_bytes=LAYER_VMEM),
         cost_estimate=pl.CostEstimate(flops=2*t*d*(4*d+2*ff)+10*t*t*d,bytes_accessed=2*d*(4*d+2*ff)+t*(30*d+6*ff),transcendentals=t*(ff+HEADS*t)),
-        )(g,mod,x,feed_out,middle,branch,u,project,*weights)
+        )(*operands[:2],mod,*operands[2:],feed_out,middle,branch,u,project,*weights)
 
 
 def matmul(left, right):
@@ -727,26 +740,24 @@
 
     forth = [(0, 1)]
     back = [(1, 0)]
-    swapped = jnp.where(first_section, total[1:], total[:1])
-    straight = jnp.where(first_section, total[:1], total[1:])
-    *_, sent = forward_layer(latents[0], total[:1], weights)
+    first, second = (latents, 0), (latents, 1)
+    straight, swapped = (0, 1), (1, 0)
+    *_, sent = forward_layer((first, first), total, (0, 0), weights)
+    inputs_one = (second, lax.ppermute(sent, "section", forth))
+    *kept_one, result_one, sent = forward_layer(inputs_one, total, swapped, weights)
     incoming = lax.ppermute(sent, "section", forth)
-    input_one = jnp.where(first_section, latents[1], incoming)
-    *kept_one, result_one, sent = forward_layer(input_one, swapped, weights)
-    incoming = lax.ppermute(sent, "section", forth)
-    *_, sent = backward_layer(cotangent[0], swapped, input_one, kept_one, weights)
+    own = (cotangent, 0)
+    *_, sent = backward_layer((own, own), total, swapped, inputs_one, kept_one, weights)
     returning = lax.ppermute(sent, "section", back)
     incoming, sent = lax.optimization_barrier((incoming, sent))
-    input_two = jnp.where(first_section, latents[0], incoming)
-    *kept_two, result_two, _ = forward_layer(input_two, straight, weights)
-    grad_result = jnp.where(first_section, returning, cotangent[1])
+    inputs_two = (first, incoming)
+    *kept_two, result_two, _ = forward_layer(inputs_two, total, straight, weights)
     mod_one, *grads_one, grad_in_one, sent = backward_layer(
-        grad_result, straight, input_two, kept_two, weights
+        (returning, (cotangent, 1)), total, straight, inputs_two, kept_two, weights
     )
     returning = lax.ppermute(sent, "section", back)
-    grad_result = jnp.where(first_section, returning, cotangent[0])
     mod_two, *grads_two, grad_in_two, _ = backward_layer(
-        grad_result, swapped, input_one, kept_one, weights
+        (returning, (cotangent, 0)), total, swapped, inputs_one, kept_one, weights
     )
 
     def products(kept, grads):

time: 570 us -> 567 us (level)
  other arithmetic: 20.8 us -> 14.1 us
    ppermute x0 -> x1, waiting for transfers between devices: none -> 12.9 us  [body(): inputs_one = (second, lax.ppermute(sent, 'section', forth))]
    ppermute x2 -> x1, waiting for transfers between devices: 12 us -> 0.01 us  [body(): incoming = lax.ppermute(sent, 'section', forth)]
    select_n x5 -> x0, other arithmetic: 6.22 us -> none  [the longest x1 1.97 us: body(): grad_result = jnp.where(first_section, returning, cotangent[0])]
  transfers between devices with their start and end apart: 4 -> 4, of which waited for: 2 -> 2; matrix products, arithmetic and copies ran while one was open for 3% -> 3% of each run, Pallas kernels for 8% -> 9%
where the time goes in v4:
time: 567 us; the launch traced here: 559 us
  Pallas kernels  496 us (87%)
  local copies, waits for them, and re-layouts  18.7 us (3%)
  other arithmetic  14.1 us (2%)
  waiting for transfers between devices  13.6 us (2%)
  starting transfers between devices  10.8 us (2%)
    pallas_call x1, Pallas kernels, reduce_all(): pl.pallas_call(functools.partial(reduce_kernel, blocks), in_specs=[any_]...  197 us
    pallas_call x1, Pallas kernels, gather_all(): pl.pallas_call(functools.partial(gather_kernel, shards, reps, arrays, chu...  155 us
    pallas_call x3, Pallas kernels, backward_layer(): pl.pallas_call(functools.partial(backward_kernel, rows, places), in_specs...  85.2 us
    pallas_call x3, Pallas kernels, forward_layer(): pl.pallas_call(functools.partial(forward_kernel, rows, places), in_specs=...  58.8 us
    ppermute x1, waiting for transfers between devices, body(): inputs_one = (second, lax.ppermute(sent, 'section', forth))  12.9 us
  transfers between devices with their start and end apart: 4, of which 2 were waited for; matrix products, arithmetic and copies ran while one was open for 3% of the time, Pallas kernels for 9%

profile of v4, /device:TPU:0, one launch (start us, length us, event | category | flops | bytes accessed | tf_op | source)
XLA Modules:
  0.0 558.6 jit_solution(10571276350014950146)
XLA Ops:
  0.6 0.7 fusion.5.refs_18_
  1.3 0.0 copy-start.18
  1.4 0.1 reshape.108
  1.4 0.6 copy.26
  2.0 154.8 %shard_map.135 = (bf16[4,4,72,3456]{3,2,1,0:T(8,128)(2,1)}, bf16[4,4,72,1152]{3,2,1,0:T(8,128)(2,1)}, bf16[4,4,72,4608]{3,2,1,0:T(8,128)(2,1)}, bf16[4,4,288,1152]{3,2,1,0:T(8,128)(2,1)}, f32[2,6912]{1,0:T(2,128)}) custom-call(bf16[4,72,3456]{2,1,0:T(8,128)(2,1)} %bitcast.85, bf16[4,72,1152]{2,1,0:T(8,128)(2,1)} %bitcast.88, bf16[4,72,4608]{2,1,0:T(8,128)(2,1)} %bitcast.77, ...), custom_call_target="tpu_custom_call" | custom-call | tf_op jit(solution)/shard_map/pallas_call | solution.py:466
  156.8 0.0 copy-done.18
  156.8 19.8 %shard_map.136 = (bf16[256,1152]{1,0:T(8,128)(2,1)}, bf16[256,3456]{1,0:T(8,128)(2,1)}, bf16[256,1152]{1,0:T(8,128)(2,1)}, f32[256,1152]{1,0:T(8,128)}, f32[256,...) custom-call(bf16[2,256,1152]{2,1,0:T(8,128)(2,1)} %x_zero.11, ...), custom_call_target="tpu_custom_call" | custom-call | flops 8455716864 | bytes 47775744 | tf_op jit(solution)/shard_map/pallas_call | solution.py:237
  176.6 3.9 collective-permute-start
  180.5 12.9 %collective-permute-done.x_one = bf16[256,1152]{1,0:T(8,128)(2,1)S(1)} collective-permute-done((bf16[256,1152]{1,0:T(8,128)(2,1)}, bf16[256,1152]{1,0:T(8,128)(2,1)S(1)}, u32[]{:S(2)}, u32[]{:S(2)}) %collective-permute-start) | collective-permute-done | bytes 589856 | tf_op jit(solution)/shard_map/ppermute | solution.py:746
  193.4 0.8 copy-done
  194.3 19.5 %shard_map.137 = (bf16[256,1152]{1,0:T(8,128)(2,1)}, bf16[256,3456]{1,0:T(8,128)(2,1)}, bf16[256,1152]{1,0:T(8,128)(2,1)}, f32[256,1152]{1,0:T(8,128)}, f32[256,...) custom-call(bf16[2,256,1152]{2,1,0:T(8,128)(2,1)} %x_zero.11, ...), custom_call_target="tpu_custom_call" | custom-call | flops 8455716864 | bytes 47775744 | tf_op jit(solution)/shard_map/pallas_call | solution.py:237
  213.8 4.3 collective-permute-start.2
  218.1 28.5 %shard_map.138 = (f32[1,6912]{1,0:T(1,128)}, bf16[256,1152]{1,0:T(8,128)(2,1)}, bf16[256,4608]{1,0:T(8,128)(2,1)}, bf16[256,1152]{1,0:T(8,128)(2,1)}, bf16[256,3...) custom-call(bf16[2,256,1152]{2,1,0:T(8,128)(2,1)} %g_one.5, bf16[2,256,1152]{2,1,0:T(8,128)(2,1)} %g_one.5, ...), custom_call_target="tpu_custom_call" | custom-call | flops 8908701696 | bytes 47775744 | tf_op jit(solution)/shard_map/pallas_call | solution.py:255
  246.6 1.3 collective-permute-start.1
  247.9 0.0 collective-permute-done.2.x_one
  247.9 0.0 copy-start.3
  247.9 0.8 copy-done.3
  248.7 19.4 %shard_map.139 = (bf16[256,1152]{1,0:T(8,128)(2,1)}, bf16[256,3456]{1,0:T(8,128)(2,1)}, bf16[256,1152]{1,0:T(8,128)(2,1)}, f32[256,1152]{1,0:T(8,128)}, f32[256,...) custom-call(bf16[2,256,1152]{2,1,0:T(8,128)(2,1)} %x_zero.11, ...), custom_call_target="tpu_custom_call" | custom-call | flops 8455716864 | bytes 47775744 | tf_op jit(solution)/shard_map/pallas_call | solution.py:237
  268.2 0.0 collective-permute-done.1.g_zero
  268.2 0.0 copy-start.15
  268.2 0.8 copy-done.15
  269.0 28.4 %shard_map.140 = (f32[1,6912]{1,0:T(1,128)}, bf16[256,1152]{1,0:T(8,128)(2,1)}, bf16[256,4608]{1,0:T(8,128)(2,1)}, bf16[256,1152]{1,0:T(8,128)(2,1)}, bf16[256,3...) custom-call(bf16[256,1152]{1,0:T(8,128)(2,1)} %copy-done.15, bf16[2,256,1152]{2,1,0:T(8,128)(2,1)} %g_one.5, ...), custom_call_target="tpu_custom_call" | custom-call | flops 8908701696 | bytes 47775744 | tf_op jit(solution)/shard_map/pallas_call | solution.py:255
  297.5 1.3 collective-permute-start.3
  298.8 0.0 copy-start.2
  298.8 4.4 copy.19
  303.2 2.4 copy.23
  305.7 1.1 copy.16
  306.7 1.1 copy.17
  307.8 1.1 copy.18
  308.9 2.3 copy.20
  311.2 0.0 copy-done.11
  311.2 1.1 copy.21
  312.3 1.1 copy.22
  313.4 0.1 select_bitcast_fusion.1
  313.5 0.7 collective-permute-done.3.g_zero
  314.2 28.3 %shard_map.141 = (f32[1,6912]{1,0:T(1,128)}, bf16[256,1152]{1,0:T(8,128)(2,1)}, bf16[256,4608]{1,0:T(8,128)(2,1)}, bf16[256,1152]{1,0:T(8,128)(2,1)}, bf16[256,3...) custom-call(bf16[256,1152]{1,0:T(8,128)(2,1)} %collective-permute-done.3.g_zero, ...), custom_call_target="tpu_custom_call" | custom-call | flops 8908701696 | bytes 47775744 | tf_op jit(solution)/shard_map/pallas_call | solution.py:255
  342.5 197.0 %shard_map.142 = (bf16[4,72,3456]{2,1,0:T(8,128)(2,1)}, bf16[4,72,1152]{2,1,0:T(8,128)(2,1)}, bf16[4,72,4608]{2,1,0:T(8,128)(2,1)}, bf16[4,4,72,1152]{3,2,1,0:T(...) custom-call(bf16[4,288,256]{2,1,0:T(8,128)(2,1)} %bitcast.92, bf16[4,288,256]{2,1,0:T(8,128)(2,1)} %bitcast.93, ...), custom_call_target="tpu_custom_call" | custom-call | flops 16307453952 | bytes 28311552 | tf_op jit(solution)/shard_map/pallas_call | solution.py:687
  539.5 0.9 slice.6
  540.4 4.9 bitcast_convert_fusion
  545.3 2.7 convert.7
  548.0 0.0 copy-done.4
  548.0 2.2 bitcast_convert_fusion.1
  550.2 1.1 bitcast_convert_fusion.2
  551.4 0.1 reshape.121
  551.5 0.6 fusion.7
  552.1 4.6 convolution_bitcast_fusion
  556.7 0.1 select_bitcast_fusion
  556.8 1.6 maximum_bitcast_fusion
  (31 shorter events, 0.1 us)
Async XLA Ops:
  1.3 155.5 %copy-start.18 = (bf16[2,1152]{1,0:T(2,128)(2,1)}, bf16[2,1152]{1,0:T(2,128)(2,1)S(1)}, u32[]{:S(2)}) copy-start(bf16[2,1152]{1,0:T(2,128)(2,1)S(1)} %fusion.5.refs_18_) | copy-start | bytes 13828
  176.6 16.8 %collective-permute-start = (bf16[256,1152]{1,0:T(8,128)(2,1)}, bf16[256,1152]{1,0:T(8,128)(2,1)S(1)}, u32[]{:S(2)}, u32[]{:S(2)}) collective-permute-start(bf16[256,1152]{1,0:T(8,128)(2,1)} %get-tuple-element.68), channel_id=1, source_target_pairs={{0,16},{1,17},{2,18},{3,19},{4,20},{5,21},{6,22},{7,23},{8,24},{9,... | collective-permute-start | bytes 1769480 | tf_op jit(solution)/shard_map/ppermute | solution.py:746
  193.4 0.8 copy-start
  213.8 34.1 %collective-permute-start.2 = (bf16[256,1152]{1,0:T(8,128)(2,1)}, bf16[256,1152]{1,0:T(8,128)(2,1)S(1)}, u32[]{:S(2)}, u32[]{:S(2)}) collective-permute-start(bf16[256,1152]{1,0:T(8,128)(2,1)} %get-tuple-element.75), channel_id=1, source_target_pairs={{0,16},{1,17},{2,18},{3,19},{4,20},{5,21},{6,22},{7,23},{8,24},{9,... | collective-permute-start | bytes 1769480 | tf_op jit(solution)/shard_map/ppermute | solution.py:748
  246.6 21.6 %collective-permute-start.1 = (bf16[256,1152]{1,0:T(8,128)(2,1)}, bf16[256,1152]{1,0:T(8,128)(2,1)S(1)}, u32[]{:S(2)}, u32[]{:S(2)}) collective-permute-start(bf16[256,1152]{1,0:T(8,128)(2,1)} %get-tuple-element.74), channel_id=1, source_target_pairs={{16,0},{17,1},{18,2},{19,3},{20,4},{21,5},{22,6},{23,7},{24,8},{25... | collective-permute-start | bytes 1769480 | tf_op jit(solution)/shard_map/ppermute | solution.py:751
  247.9 0.8 copy-start.3
  268.2 0.8 copy-start.15
  297.5 16.7 %collective-permute-start.3 = (bf16[256,1152]{1,0:T(8,128)(2,1)}, bf16[256,1152]{1,0:T(8,128)(2,1)}, u32[]{:S(2)}, u32[]{:S(2)}) collective-permute-start(bf16[256,1152]{1,0:T(8,128)(2,1)} %get-tuple-element.84), channel_id=1, source_target_pairs={{16,0},{17,1},{18,2},{19,3},{20,4},{21,5},{22,6},{23,7},{24,8},{25... | collective-permute-start | bytes 1769480 | tf_op jit(solution)/shard_map/ppermute | solution.py:758
  298.8 4.4 copy-start.2
  303.2 2.4 copy-start.14
  303.2 3.5 copy-start.13
  305.6 2.2 copy-start.12
  306.7 4.4 copy-start.11
  307.8 4.4 copy-start.10
  308.9 4.5 copy-start.6
  308.9 4.5 copy-start.8
  540.4 4.9 copy-start.1
  545.3 2.7 copy-start.4
  548.0 2.2 copy-start.9
  550.2 1.2 copy-start.19
  550.2 1.3 copy-start.17
  550.2 1.9 copy-start.16
  552.1 4.6 copy-start.5
  552.1 4.6 copy-start.7
